TPU v7x, 32 devices: a 4x4x1 block of a 4x4x8 slice. The times are simulated.
32 devices in a mesh: stage: 1 (over z), data: 32 (over y, x, core).
Axes of the slice: x: 4, y: 4, z: 1, core: 2. Of those that a mesh axis runs over, the one named last changes fastest.
The devices are a block of a 4x4x8 slice.
Arguments:
- grad_attn: float32 [32, 1, 2048, 2048], P(('stage', 'data'))
- mom_attn: float32 [1, 2048, 2048], P('stage', 'data')
- master_attn: float32 [1, 2048, 2048], P('stage', 'data')
- grad_up: float32 [32, 1, 2048, 1024], P(('stage', 'data'))
- mom_up: float32 [1, 2048, 1024], P('stage', 'data')
- master_up: float32 [1, 2048, 1024], P('stage', 'data')
- grad_down: float32 [32, 1, 1024, 2048], P(('stage', 'data'))
- mom_down: float32 [1, 1024, 2048], P('stage', 'data')
- master_down: float32 [1, 1024, 2048], P('stage', 'data')
Outputs:
- output 1: float32 [1, 2048, 2048], P('stage', 'data')
- output 2: float32 [1, 2048, 2048], P('stage', 'data')
- output 3: bfloat16 [1, 2048, 2048], P('stage', 'data')
- output 4: float32 [1, 2048, 1024], P('stage', 'data')
- output 5: float32 [1, 2048, 1024], P('stage', 'data')
- output 6: bfloat16 [1, 2048, 1024], P('stage', 'data')
- output 7: float32 [1, 1024, 2048], P('stage', 'data')
- output 8: float32 [1, 1024, 2048], P('stage', 'data')
- output 9: bfloat16 [1, 1024, 2048], P('stage', 'data')
All inputs are finite; a program needn't handle non-finite values.
Results may differ from a plain program's by a relative error of at most 0.0070479.
Values are sent between devices in bfloat16 or wider.
A program may use at most 768 MiB of HBM per device.

v0:
```python
import math
import functools
import jax
import jax.numpy as jnp
from jax import lax
from jax.sharding import PartitionSpec as P, NamedSharding

MOMENTUM = 0.95
LEARN_RATE = 0.25
WEIGHT_DECAY = 0.2
EPSILON = 1e-7
COEF_A = 3.4445
COEF_B = -4.7750
COEF_C = 2.0315
NS_STEPS = 5


def newton_schulz(x_mat, is_tall):
    for _ in range(NS_STEPS):
        if is_tall:
            gram_mat = jnp.einsum('bkr,bkc->brc', x_mat, x_mat, preferred_element_type=jnp.float32)
        else:
            gram_mat = jnp.einsum('brk,bck->brc', x_mat, x_mat, preferred_element_type=jnp.float32)
        gram_mat = gram_mat.astype(jnp.bfloat16)
        gram_sq = jnp.einsum('brk,bkc->brc', gram_mat, gram_mat, preferred_element_type=jnp.float32).astype(jnp.bfloat16)
        poly_mat = (COEF_B * gram_mat.astype(jnp.float32) + COEF_C * gram_sq.astype(jnp.float32)).astype(jnp.bfloat16)
        if is_tall:
            update = jnp.einsum('bkc,brc->bkr', x_mat, poly_mat, preferred_element_type=jnp.float32)
        else:
            update = jnp.einsum('brc,bck->brk', poly_mat, x_mat, preferred_element_type=jnp.float32)
        x_mat = (COEF_A * x_mat.astype(jnp.float32) + update.astype(jnp.bfloat16).astype(jnp.float32)).astype(jnp.bfloat16)
    return x_mat


def stack_step(grad_all, mom_old, master_old, offset, group_size):
    count, rows_local, n_cols = mom_old.shape
    n_rows = rows_local * group_size
    grad_rows = lax.psum_scatter(grad_all[0], 'data', scatter_dimension=1, tiled=True) / group_size
    mom_new = MOMENTUM * mom_old + grad_rows
    norm_sq = lax.psum(jnp.sum(mom_new * mom_new, axis=(1, 2)), 'data')
    x_rows = (mom_new / (jnp.sqrt(norm_sq)[:, None, None] + EPSILON)).astype(jnp.bfloat16)
    slots = (count + offset + group_size - 1) // group_size
    padded = jnp.pad(x_rows, ((offset, slots * group_size - count - offset), (0, 0), (0, 0)))
    send_buf = padded.reshape(slots, group_size, rows_local, n_cols)
    owned = lax.all_to_all(send_buf, 'data', 1, 2, tiled=True).reshape(slots, n_rows, n_cols)
    positions = jnp.arange(slots) * group_size + lax.axis_index('data')
    has_work = jnp.any((positions >= offset) & (positions < offset + count))
    ortho_mat = lax.cond(has_work, functools.partial(newton_schulz, is_tall=n_rows > n_cols), jnp.zeros_like, owned)
    returned = lax.all_to_all(ortho_mat.reshape(slots, 1, n_rows, n_cols), 'data', 2, 1, tiled=True)
    ortho_rows = returned.reshape(slots * group_size, rows_local, n_cols)[offset:offset + count]
    scale = 0.2 * math.sqrt(max(n_rows, n_cols))
    master_new = master_old - LEARN_RATE * (scale * ortho_rows.astype(jnp.float32) + WEIGHT_DECAY * master_old)
    return [mom_new, master_new, master_new.astype(jnp.bfloat16)]


def solution(mesh):
    group_size = mesh.shape['data']
    grad_spec = P(('stage', 'data'), None, None, None)
    row_spec = P('stage', 'data', None)

    def step_local(*arrays):
        attn_count = arrays[1].shape[0]
        expert_count = arrays[4].shape[0]
        offsets = (0, attn_count % group_size, (attn_count + expert_count) % group_size)
        results = []
        for stack_idx in range(3):
            results.extend(stack_step(arrays[3 * stack_idx], arrays[3 * stack_idx + 1], arrays[3 * stack_idx + 2], offsets[stack_idx], group_size))
        return tuple(results)

    in_specs = (grad_spec, row_spec, row_spec) * 3
    out_specs = (row_spec,) * 9
    return jax.shard_map(step_local, mesh=mesh, in_specs=in_specs, out_specs=out_specs, check_vma=False)
```

profile of v0, /device:TPU:97, one launch (start us, length us, event | category | flops | bytes accessed | tf_op | source)
XLA Modules:
  0.0 1324.5 jit_solution(8718518694969506651)
XLA Ops:
  9.6 89.1 %reduce-scatter.6.cloned.1.call-done = f32[1,64,1024]{2,1,0:T(8,128)} async-done(((f32[1,2048,1024]{2,1,0:T(8,128)}), f32[1,64,1024]{2,1,0:T(8,128)}) %reduce-scatter.6.cloned.1.call-update) | async-done | bytes 262160 | tf_op jit(solution)/shard_map/reduce_scatter | solution.py:38
  100.4 86.3 %reduce-scatter.8.cloned.1.call-done = f32[1,32,2048]{2,1,0:T(8,128)} async-done(((f32[1,1024,2048]{2,1,0:T(8,128)}), f32[1,32,2048]{2,1,0:T(8,128)}) %reduce-scatter.8.cloned.1.call-update) | async-done | bytes 262160 | tf_op jit(solution)/shard_map/reduce_scatter | solution.py:38
  188.3 109.2 %reduce-scatter.4.cloned.1.call-done = f32[1,64,2048]{2,1,0:T(8,128)} async-done(((f32[1,2048,2048]{2,1,0:T(8,128)}), f32[1,64,2048]{2,1,0:T(8,128)}) %reduce-scatter.4.cloned.1.call-update) | async-done | bytes 524304 | tf_op jit(solution)/shard_map/reduce_scatter | solution.py:38
  299.3 46.3 %all-reduce.3 = (f32[1]{0:T(128)}, f32[1]{0:T(128)}, f32[1]{0:T(128)}) all-reduce(f32[1]{0:T(128)} %bitcast.16, f32[1]{0:T(128)} %bitcast.22, f32[1]{0:T(128)} %bitcast.28), channel_id=1, replica_groups=mesh['stage'=1,'data'=32] {'data'}, use_global_device_ids=true, to_apply=%region_2.0 | all-reduce | flops 3 | bytes 24 | tf_op jit(solution)/shard_map/psum | solution.py:40
  346.3 2.5 pad_bitcast_fusion.1
  348.8 4.4 all-to-all-start.4
  353.9 2.5 pad_bitcast_fusion.2
  356.4 48.2 %all-to-all-done.4 = bf16[1,32,32,2048]{3,2,0,1:T(8,128)(2,1)} async-done(((bf16[1,32,32,2048]{3,2,0,1:T(8,128)(2,1)}), bf16[1,32,32,2048]{3,2,0,1:T(8,128)(2,1)}, u32[]{:S(2)}, u32[]{:S(2)}) %all-to-all-start.4) | async-done | bytes 4194336 | tf_op jit(solution)/shard_map/all_to_all | solution.py:45
  404.6 9.5 all-to-all-start.2
  414.8 4.3 pad_bitcast_fusion
  419.1 47.5 %all-to-all-done.2 = bf16[1,32,64,1024]{3,2,0,1:T(8,128)(2,1)} async-done(((bf16[1,32,64,1024]{3,2,0,1:T(8,128)(2,1)}), bf16[1,32,64,1024]{3,2,0,1:T(8,128)(2,1)}, u32[]{:S(2)}, u32[]{:S(2)}) %all-to-all-start.2) | async-done | bytes 4194336 | tf_op jit(solution)/shard_map/all_to_all | solution.py:45
  466.6 8.1 all-to-all-start
  474.7 6.2 conditional.5
  474.7 2.5 broadcast.113
  481.0 8.7 copy.63
  490.2 26.7 %reduce.5 = bf16[1024,2048]{1,0:T(8,128)(2,1)} reduce(bf16[1024,1,1,2048]{3,2,1,0:T(2,128)(2,1)} %bitcast.180, bf16[]{:T(256)} %broadcast.280), dimensions={1,2}, to_apply=%bitcast.176.reduce_sub_computation | reduce | bytes 8388610
  516.9 7.8 reshape.606
  524.6 54.5 %all-to-all-done = bf16[1,32,64,2048]{3,2,0,1:T(8,128)(2,1)} async-done(((bf16[1,32,64,2048]{3,2,0,1:T(8,128)(2,1)}), bf16[1,32,64,2048]{3,2,0,1:T(8,128)(2,1)}, u32[]{:S(2)}, u32[]{:S(2)}) %all-to-all-start) | async-done | bytes 8388640 | tf_op jit(solution)/shard_map/all_to_all | solution.py:45
  579.1 40.8 %all-to-all-start.5 = ((bf16[32,2,32768]{2,1,0:T(2,128)(2,1)}), bf16[32,2,32768]{2,1,0:T(2,128)(2,1)}, u32[]{:S(2)}, u32[]{:S(2)}) async-start(bf16[32,2,32768]{2,1,0:T(2,128)(2,1)} %reshape.606), calls=%async_computation.8 | async-start | bytes 8388608 | tf_op jit(solution)/shard_map/all_to_all | solution.py:49
  619.9 105.4 %conditional.4 = (bf16[1,2048,1024]{1,2,0:T(8,128)(2,1)}) conditional(s32[]{:T(128)} %convert_element_type.629, () %tuple.27, bf16[1,32,64,1024]{3,2,0,1:T(8,128)(2,1)} %all-to-all-done.2), branch_computations={%region_8.9_spmd, %region_9.10_spmd} | conditional | flops 53791948800 | bytes 96469000 | solution.py:48
  620.1 6.5 copy.39
  626.6 8.0 bitcast_convert_fusion
  634.7 11.1 fusion.41
  645.8 8.0 convolution_convert_fusion.8
  653.8 11.9 add_convert_fusion.28
  665.8 8.0 convolution_convert_fusion.7
  673.8 11.7 add_convert_fusion.27
  685.4 8.0 convolution_convert_fusion.6
  693.4 12.1 add_convert_fusion.26
  705.5 8.0 convolution_convert_fusion.5
  713.5 11.7 fusion.42
  725.4 20.6 %copy.48 = bf16[1,1,2048,1024]{3,1,0,2:T(2,128)(2,1)} copy(bf16[1,1,2048,1024]{2,3,1,0:T(8,128)(2,1)} %bitcast.185) | data formatting | bytes 8388608 | tf_op jit(solution)/shard_map/reshape | solution.py:49
  746.0 26.0 %reduce.4 = bf16[2048,1024]{1,0:T(8,128)(2,1)} reduce(bf16[2048,1,1,1024]{3,2,1,0:T(2,128)(2,1)} %bitcast.181, bf16[]{:T(256)} %broadcast.280), dimensions={1,2}, to_apply=%bitcast.67.reduce_sub_computation | reduce | bytes 8388610
  771.9 7.8 reshape.604
  779.8 3.8 all-to-all-start.3
  783.5 8.1 conditional.3
  783.5 4.3 broadcast.105
  791.6 15.5 %copy.62 = bf16[1,1,2048,2048]{3,1,0,2:T(2,128)(2,1)} copy(bf16[1,1,2048,2048]{3,2,1,0:T(8,128)(2,1)} %bitcast.179) | data formatting | bytes 16777216 | tf_op jit(solution)/shard_map/reshape | solution.py:49
  807.1 51.0 %reduce.3 = bf16[2048,2048]{1,0:T(8,128)(2,1)} reduce(bf16[2048,1,1,2048]{3,2,1,0:T(2,128)(2,1)} %bitcast.178, bf16[]{:T(256)} %broadcast.280), dimensions={1,2}, to_apply=%bitcast.175.reduce_sub_computation | reduce | bytes 16777218
  858.1 21.6 %reshape.602 = bf16[32,2,65536]{2,1,0:T(2,128)(2,1)} reshape(bf16[2048,2048]{1,0:T(8,128)(2,1)} %reduce.3) | data formatting | bytes 16777216
  879.8 294.9 %all-to-all-start.1 = ((bf16[32,2,65536]{2,1,0:T(2,128)(2,1)}), bf16[32,2,65536]{2,1,0:T(2,128)(2,1)}, u32[]{:S(2)}, u32[]{:S(2)}) async-start(bf16[32,2,65536]{2,1,0:T(2,128)(2,1)} %reshape.602), calls=%async_computation.2 | async-start | bytes 16777216 | tf_op jit(solution)/shard_map/all_to_all | solution.py:49
  1174.7 19.8 %reshape.607 = bf16[1024,1,1,2048]{3,2,1,0:T(2,128)(2,1)} reshape(bf16[32,2,32768]{2,1,0:T(2,128)(2,1)} %all-to-all-done.5) | data formatting | bytes 8388608
  1194.5 8.0 copy.59
  1202.4 19.8 %reshape.605 = bf16[2048,1,1,1024]{3,2,1,0:T(2,128)(2,1)} reshape(bf16[32,2,32768]{2,1,0:T(2,128)(2,1)} %all-to-all-done.3) | data formatting | bytes 8388608
  1222.2 5.1 copy.58
  1229.9 51.3 %all-to-all-done.1 = bf16[32,2,65536]{2,1,0:T(2,128)(2,1)} async-done(((bf16[32,2,65536]{2,1,0:T(2,128)(2,1)}), bf16[32,2,65536]{2,1,0:T(2,128)(2,1)}, u32[]{:S(2)}, u32[]{:S(2)}) %all-to-all-start.1) | async-done | bytes 8388640 | tf_op jit(solution)/shard_map/all_to_all | solution.py:49
  1281.2 23.4 %reshape.603 = bf16[2048,1,1,2048]{3,2,1,0:T(2,128)(2,1)} reshape(bf16[32,2,65536]{2,1,0:T(2,128)(2,1)} %all-to-all-done.1) | data formatting | bytes 16777216
  1304.6 11.8 copy.57
  (36 shorter events, 11.5 us)
Async XLA Ops:
  7.2 91.5 %reduce-scatter.6.cloned.1.call-start = ((), (), s32[]{:S(2)}) async-start(), calls=%async_computation.10 | async-start | bytes 8650752 | tf_op jit(solution)/shard_map/reduce_scatter | solution.py:38
  8.0 178.7 %reduce-scatter.8.cloned.1.call-start = ((), (), s32[]{:S(2)}) async-start(), calls=%async_computation.11 | async-start | bytes 8650752 | tf_op jit(solution)/shard_map/reduce_scatter | solution.py:38
  8.8 288.7 %reduce-scatter.4.cloned.1.call-start = ((), (), s32[]{:S(2)}) async-start(), calls=%async_computation.9 | async-start | bytes 17301504 | tf_op jit(solution)/shard_map/reduce_scatter | solution.py:38
  8.9 89.9 %copy-start.7 = (f32[1,64,1024]{2,1,0:T(8,128)S(1)}, f32[1,64,1024]{2,1,0:T(8,128)}, u32[]{:S(2)}) copy-start(f32[1,64,1024]{2,1,0:T(8,128)} %param.19) | copy-start | bytes 786436
  8.9 177.8 %copy-start.8 = (f32[1,32,2048]{2,1,0:T(8,128)S(1)}, f32[1,32,2048]{2,1,0:T(8,128)}, u32[]{:S(2)}) copy-start(f32[1,32,2048]{2,1,0:T(8,128)} %param.22) | copy-start | bytes 786436
  8.9 288.6 %copy-start.4 = (f32[1,64,2048]{2,1,0:T(8,128)S(1)}, f32[1,64,2048]{2,1,0:T(8,128)}, u32[]{:S(2)}) copy-start(f32[1,64,2048]{2,1,0:T(8,128)} %param.16) | copy-start | bytes 1572868
  100.4 253.5 %copy-start.1 = (f32[1,64,1024]{2,1,0:T(8,128)}, f32[1,64,1024]{2,1,0:T(8,128)S(1)}, u32[]{:S(2)}) copy-start(f32[1,64,1024]{2,1,0:T(8,128)S(1)} %get-tuple-element.36) | copy-start | bytes 786436
  188.3 160.5 %copy-start.2 = (f32[1,32,2048]{2,1,0:T(8,128)}, f32[1,32,2048]{2,1,0:T(8,128)S(1)}, u32[]{:S(2)}) copy-start(f32[1,32,2048]{2,1,0:T(8,128)S(1)} %get-tuple-element.34) | copy-start | bytes 786436
  299.3 115.5 %copy-start = (f32[1,64,2048]{2,1,0:T(8,128)}, f32[1,64,2048]{2,1,0:T(8,128)S(1)}, u32[]{:S(2)}) copy-start(f32[1,64,2048]{2,1,0:T(8,128)S(1)} %get-tuple-element.38) | copy-start | bytes 1572868
  348.8 55.8 %all-to-all-start.4 = ((bf16[1,32,32,2048]{3,2,0,1:T(8,128)(2,1)}), bf16[1,32,32,2048]{3,2,0,1:T(8,128)(2,1)}, u32[]{:S(2)}, u32[]{:S(2)}) async-start(bf16[1,32,32,2048]{3,2,0,1:T(8,128)(2,1)} %pad_bitcast_fusion.1), calls=%async_computation.7 | async-start | bytes 8388608 | tf_op jit(solution)/shard_map/all_to_all | solution.py:45
  404.6 62.0 %all-to-all-start.2 = ((bf16[1,32,64,1024]{3,2,0,1:T(8,128)(2,1)}), bf16[1,32,64,1024]{3,2,0,1:T(8,128)(2,1)}, u32[]{:S(2)}, u32[]{:S(2)}) async-start(bf16[1,32,64,1024]{3,2,0,1:T(8,128)(2,1)} %pad_bitcast_fusion.2), calls=%async_computation.4 | async-start | bytes 8388608 | tf_op jit(solution)/shard_map/all_to_all | solution.py:45
  466.6 112.5 %all-to-all-start = ((bf16[1,32,64,2048]{3,2,0,1:T(8,128)(2,1)}), bf16[1,32,64,2048]{3,2,0,1:T(8,128)(2,1)}, u32[]{:S(2)}, u32[]{:S(2)}) async-start(bf16[1,32,64,2048]{3,2,0,1:T(8,128)(2,1)} %pad_bitcast_fusion), calls=%async_computation.1 | async-start | bytes 16777216 | tf_op jit(solution)/shard_map/all_to_all | solution.py:45
  579.1 200.6 %all-to-all-start.5 = ((bf16[32,2,32768]{2,1,0:T(2,128)(2,1)}), bf16[32,2,32768]{2,1,0:T(2,128)(2,1)}, u32[]{:S(2)}, u32[]{:S(2)}) async-start(bf16[32,2,32768]{2,1,0:T(2,128)(2,1)} %reshape.606), calls=%async_computation.8 | async-start | bytes 8388608 | tf_op jit(solution)/shard_map/all_to_all | solution.py:49
  779.8 100.0 %all-to-all-start.3 = ((bf16[32,2,32768]{2,1,0:T(2,128)(2,1)}), bf16[32,2,32768]{2,1,0:T(2,128)(2,1)}, u32[]{:S(2)}, u32[]{:S(2)}) async-start(bf16[32,2,32768]{2,1,0:T(2,128)(2,1)} %reshape.604), calls=%async_computation.5 | async-start | bytes 8388608 | tf_op jit(solution)/shard_map/all_to_all | solution.py:49
  879.8 401.5 %all-to-all-start.1 = ((bf16[32,2,65536]{2,1,0:T(2,128)(2,1)}), bf16[32,2,65536]{2,1,0:T(2,128)(2,1)}, u32[]{:S(2)}, u32[]{:S(2)}) async-start(bf16[32,2,65536]{2,1,0:T(2,128)(2,1)} %reshape.602), calls=%async_computation.2 | async-start | bytes 16777216 | tf_op jit(solution)/shard_map/all_to_all | solution.py:49
  1222.2 5.1 copy-start.5
  1222.2 6.0 copy-start.6
  1304.6 11.8 copy-start.3
Sparse Core Ops, SparseCore 0:
  11.6 87.1 reduce-scatter.5
  102.3 84.3 reduce-scatter.7
  190.5 106.9 reduce-scatter.3
where the time goes:
time: 1340 us; the launch traced here: 1320 us
  waiting for transfers between devices  488 us (36%)
  starting transfers between devices  362 us (27%)
  local copies, waits for them, and re-layouts  193 us (14%)
  other arithmetic  112 us (8%)
  matrix products  98.5 us (7%)
  blocking collectives  46.3 us (3%)
  between operations  16.6 us (1%)
    all_to_all x3, starting transfers between devices, stack_step(): lax.all_to_all(ortho_mat.reshape(slots, 1, n_rows, n_cols), 'data', 2, 1,...  339 us
    reduce_scatter x3, waiting for transfers between devices, stack_step(): lax.psum_scatter(grad_all[0], 'data', scatter_dimension=1, tiled=True)  285 us
    all_to_all x3, waiting for transfers between devices, stack_step(): lax.all_to_all(send_buf, 'data', 1, 2, tiled=True)  150 us
    unnamed x28, local copies, waits for them, and re-layouts  126 us
    unnamed x3, other arithmetic  104 us
    dot_general x5, matrix products, newton_schulz(): jnp.einsum('bkc,brc->bkr', x_mat, poly_mat, preferred_element_type=jnp.fl...  58.5 us
    all_to_all x3, waiting for transfers between devices, stack_step(): lax.all_to_all(ortho_mat.reshape(slots, 1, n_rows, n_cols), 'data', 2, 1,...  51.3 us
    psum x1, blocking collectives, stack_step(): norm_sq = lax.psum(jnp.sum(mom_new * mom_new, axis=(1, 2)), 'data')  46.3 us
  transfers between devices with their start and end apart: 9, of which 7 were waited for; matrix products, arithmetic and copies ran while one was open for 27% of the time, Pallas kernels for 0%

commit v1 on v0

v1 whole, which is shorter than its diff:
```python
import functools
import math

import jax
import jax.numpy as jnp
from jax import lax
from jax.experimental import pallas as pl
from jax.experimental.pallas import tpu as pltpu
from jax.sharding import PartitionSpec as P

MOMENTUM = 0.95
LEARN_RATE = 0.25
WEIGHT_DECAY = 0.2
EPSILON = 1e-7
COEF_A = 3.4445
COEF_B = -4.7750
COEF_C = 2.0315
NS_STEPS = 5
F32 = jnp.float32
BF16 = jnp.bfloat16
MESH = pl.DeviceIdType.MESH
VMEM_LIMIT = 66_000_000


def ns_kernel(n, ax, xa, xu, xd, wa, wu, wd, wa_n, wa_b, wu_n, wu_b, wd_n, wd_b,
              X, A, B, stage, obuf, oa, ou, od, load_sem, asend, arecv, bsend, brecv, xsend, xrecv, osend, orecv):
    me = lax.axis_index(ax)
    role = lax.rem(me, 4)
    base = me - role
    blk = n // 4
    half = n // 2

    def dev(k):
        return {ax: k}

    barrier = pltpu.get_barrier_semaphore()
    for step in range(1, 4):
        pl.semaphore_signal(barrier, inc=1, device_id=dev(base + lax.rem(role + step, 4)), device_id_type=MESH)
    pl.semaphore_wait(barrier, 3)

    def at(ref, i, j):
        return ref.at[pl.ds(pl.multiple_of(i * blk, blk), blk), pl.ds(pl.multiple_of(j * blk, blk), blk)]

    def rows(i, size=blk):
        return pl.ds(pl.multiple_of(i * size, size), size)

    def poly(a, q):
        return (COEF_B * a.astype(F32) + COEF_C * q.astype(BF16).astype(F32)).astype(BF16)

    def blend(x, y):
        return (COEF_A * x.astype(F32) + y.astype(BF16).astype(F32)).astype(BF16)

    def dot_nt(a, b):
        return lax.dot_general(a, b, (((1,), (1,)), ((), ())), preferred_element_type=F32)

    def dot(a, b):
        return jnp.dot(a, b, preferred_element_type=F32)

    @pl.when(role < 2)
    def _():
        c = role
        peer = dev(base + 1 - c)
        p_own, s_own = 3 * c, 1 + c
        p_peer, s_peer = 3 - 3 * c, 2 - c
        i1, j1 = 1 + 2 * c, 3 - 3 * c
        i2, j2 = 2 * c, 2 - c

        loads = [pltpu.make_async_copy(xa.at[rows(p)], X.at[0, rows(p)], load_sem.at[k])
                 for k, p in enumerate((p_own, s_own, p_peer, s_peer))]
        for cp in loads:
            cp.start()
        for cp in loads:
            cp.wait()

        def a_copy(k, i, j):
            return pltpu.make_async_remote_copy(at(A, i, j), at(A, i, j), asend.at[k], arecv.at[k],
                                                device_id=peer, device_id_type=MESH)

        a_blocks = ((p_own, p_own), (p_own, s_own), (s_own, p_own), (i1, j1), (j1, i1), (i2, j2), (j2, i2), (s_own, s_own))

        def a_send(k):
            a_copy(k, *a_blocks[k]).start()

        def a_wait(*ks):
            for k in ks:
                a_copy(k, *a_blocks[k]).wait_recv()

        def x_copy(nxt, p, j, k):
            ref = at(X.at[nxt], p, j)
            return pltpu.make_async_remote_copy(ref, ref, xsend.at[k, j], xrecv.at[k, j],
                                                device_id=peer, device_id_type=MESH)

        def x_wait(cur, k):
            for j in range(4):
                x_copy(cur, (p_peer, s_peer)[k], j, k).wait_recv()

        def b_copy(k):
            i, j = ((i1, j1), (i2, j2))[k]
            return pltpu.make_async_remote_copy(stage.at[k], at(B, j - 2 * (1 - c), i), bsend.at[k], brecv.at[k],
                                                device_id=peer, device_id_type=MESH)

        def gram(xt, i, j, mirror):
            v = dot_nt(xt[rows(i), :], xt[rows(j), :]).astype(BF16)
            at(A, i, j)[...] = v
            if mirror:
                at(A, j, i)[...] = v.T

        def a_step(t, cur):
            xt = X.at[cur]
            gram(xt, p_own, p_own, False)

            @pl.when(t > 0)
            def _():
                x_wait(cur, 0)
            a_send(0)
            gram(xt, p_own, s_own, True)
            a_send(1)
            a_send(2)
            gram(xt, i1, j1, True)
            a_send(3)
            a_send(4)

            @pl.when(t > 0)
            def _():
                x_wait(cur, 1)
            gram(xt, i2, j2, True)
            a_send(5)
            a_send(6)
            gram(xt, s_own, s_own, False)
            a_send(7)

        def x_wait_send(nxt):
            for k, p in enumerate((p_own, s_own)):
                for j in range(4):
                    x_copy(nxt, p, j, k).wait_send()

        def q_block(i, j):
            q = dot(A[rows(i), :], A[:, pl.ds(pl.multiple_of(j * blk, blk), blk)])
            v = poly(at(A, i, j)[...], q)
            at(B, i - 2 * c, j)[...] = v
            return v

        def q_step(t, cur):
            a_wait(3, 4)
            q_block(p_own, p_own)
            a_wait(5, 6)
            v = q_block(p_own, s_own)
            at(B, s_own - 2 * c, p_own)[...] = v.T
            a_wait(0, 1, 2)
            v = q_block(i1, j1)
            stage[0] = v.T
            b_copy(0).start()
            a_wait(7)
            v = q_block(i2, j2)
            stage[1] = v.T
            b_copy(1).start()
            q_block(s_own, s_own)
            for k in range(8):
                a_copy(k, *a_blocks[k]).wait_send()

            @pl.when(t > 0)
            def _():
                x_wait_send(cur)

        def y_step(cur, nxt):
            xt, xn = X.at[cur], X.at[nxt]
            for k, p in enumerate((p_own, s_own)):
                b_copy(k).wait_recv()

                @pl.loop(0, 4)
                def _(j):
                    cols = pl.ds(pl.multiple_of(j * blk, blk), blk)
                    y = dot(B[rows(p - 2 * c), :], xt[:, cols])
                    at(xn, p, j)[...] = blend(at(xt, p, j)[...], y)
                    x_copy(nxt, p, j, k).start()
            for k in range(2):
                b_copy(k).wait_send()

        @pl.loop(0, NS_STEPS - 1)
        def _(t):
            cur = lax.rem(t, 2)
            nxt = 1 - cur
            a_step(t, cur)
            q_step(t, cur)
            y_step(cur, nxt)

        last = NS_STEPS - 1
        cur = last % 2
        a_step(last, cur)
        a_wait(*range(8))
        for k in range(8):
            a_copy(k, *a_blocks[k]).wait_send()
        x_wait_send(cur)
        own = oa.shape[0]
        mine = pl.ds(pl.multiple_of(own * (base + 2 * c), 2 * own), 2 * own)
        for j in range(4):
            cols = pl.ds(j * blk, blk)
            B[0:2 * own, cols] = poly(A[mine, cols], dot(A[mine, :], A[:, cols]))
        for j in range(4):
            cols = pl.ds(j * blk, blk)
            obuf[0:2 * own, cols] = blend(X[cur, mine, cols], dot(B[0:2 * own, :], X[cur, :, cols]))

        def o_copy(k, target):
            return pltpu.make_async_remote_copy(obuf.at[pl.ds(own * k, own)], oa, osend.at[k], orecv.at[0],
                                                device_id=dev(target), device_id_type=MESH)

        @pl.when(c == 1)
        def _():
            o_copy(0, base + 2).start()
            o_copy(1, base + 3).start()
            o_copy(0, base + 2).wait_send()
            o_copy(1, base + 3).wait_send()

        @pl.when(c == 0)
        def _():
            o_copy(1, base + 1).start()
            oa[...] = obuf[0:own, :]
            o_copy(1, base + 1).wait_send()

    @pl.when(role >= 2)
    def _():
        @pl.when(role == 2)
        def _():
            cp = pltpu.make_async_copy(xu, X.at[1, :, pl.ds(0, half)], load_sem.at[0])
            cp.start()
            cp.wait()

            @pl.loop(0, 4)
            def _(i):
                for j in range(2):
                    at(X.at[0], j, i)[...] = at(X.at[1], i, j)[...].T

        @pl.when(role == 3)
        def _():
            cp = pltpu.make_async_copy(xd, X.at[0, pl.ds(0, half)], load_sem.at[0])
            cp.start()
            cp.wait()

        def a_step(cur):
            @pl.loop(0, 2)
            def _(i):
                for j in range(2):
                    at(A, i, j)[...] = dot_nt(X[cur, rows(i), :], X[cur, j * blk:(j + 1) * blk, :]).astype(BF16)

        def q_rows(i):
            for j in range(2):
                q = dot(A[rows(i), 0:half], A[0:half, j * blk:(j + 1) * blk])
                at(B, i, j)[...] = poly(at(A, i, j)[...], q)

        @pl.loop(0, NS_STEPS - 1)
        def _(t):
            cur = lax.rem(t, 2)
            nxt = 1 - cur
            a_step(cur)

            @pl.loop(0, 2)
            def _(i):
                q_rows(i)

            @pl.loop(0, 4)
            def _(j):
                cols = pl.ds(pl.multiple_of(j * blk, blk), blk)
                for i in range(2):
                    y = dot(B[i * blk:(i + 1) * blk, 0:half], X[cur, 0:half, cols])
                    at(X.at[nxt], i, j)[...] = blend(at(X.at[cur], i, j)[...], y)

        cur = (NS_STEPS - 1) % 2
        a_step(cur)

        @pl.when(role == 2)
        def _():
            own = ou.shape[0]
            cols = pl.ds(pl.multiple_of(own * base, 4 * own), 4 * own)
            for i in range(2):
                q_rows(i)
            for i in range(2):
                o = blend(X[cur, i * blk:(i + 1) * blk, cols], dot(B[i * blk:(i + 1) * blk, 0:half], X[cur, 0:half, cols]))
                obuf[0:4 * own, i * blk:(i + 1) * blk] = o.T

            def o_copy(k):
                return pltpu.make_async_remote_copy(obuf.at[pl.ds(own * k, own), pl.ds(0, half)], ou, osend.at[k], orecv.at[1],
                                                    device_id=dev(base + k), device_id_type=MESH)
            for k in (0, 1, 3):
                o_copy(k).start()
            ou[...] = obuf[2 * own:3 * own, 0:half]
            for k in (0, 1, 3):
                o_copy(k).wait_send()

        @pl.when(role == 3)
        def _():
            own = od.shape[0]
            mine = pl.ds(pl.multiple_of(own * base, 4 * own), 4 * own)
            for j in range(2):
                cols = pl.ds(j * blk, blk)
                B[0:4 * own, cols] = poly(A[mine, cols], dot(A[mine, 0:half], A[0:half, cols]))
            for j in range(4):
                cols = pl.ds(j * blk, blk)
                obuf[0:4 * own, cols] = blend(X[cur, mine, cols], dot(B[0:4 * own, 0:half], X[cur, 0:half, cols]))

            def o_copy(k):
                return pltpu.make_async_remote_copy(obuf.at[pl.ds(own * k, own)], od, osend.at[k], orecv.at[2],
                                                    device_id=dev(base + k), device_id_type=MESH)
            for k in (0, 1, 2):
                o_copy(k).start()
            od[...] = obuf[3 * own:4 * own, :]
            for k in (0, 1, 2):
                o_copy(k).wait_send()

    def update(o, w, w_n, w_b, scale):
        old = w[...]
        new = old - LEARN_RATE * (scale * o[...].astype(F32) + WEIGHT_DECAY * old)
        w_n[...] = new
        w_b[...] = new.astype(BF16)

    def arrived(o, k):
        pltpu.make_async_remote_copy(o, o, osend.at[k], orecv.at[k], device_id=dev(base), device_id_type=MESH).wait_recv()

    scale = 0.2 * math.sqrt(n)

    @pl.when(role != 3)
    def _():
        arrived(od, 2)
    update(od, wd, wd_n, wd_b, scale)

    @pl.when(role != 2)
    def _():
        arrived(ou, 1)
    update(ou, wu, wu_n, wu_b, scale)

    @pl.when(role != 0)
    def _():
        arrived(oa, 0)
    update(oa, wa, wa_n, wa_b, scale)


def orthogonalize(ax, xa, xu, xd, wa, wu, wd):
    n = xa.shape[1]
    blk = n // 4
    dma = pltpu.SemaphoreType.DMA
    vmem = pl.BlockSpec(memory_space=pltpu.VMEM)
    hbm = pl.BlockSpec(memory_space=pl.ANY)
    outs = []
    for w in (wa, wu, wd):
        outs += [jax.ShapeDtypeStruct(w.shape, F32), jax.ShapeDtypeStruct(w.shape, BF16)]
    return pl.pallas_call(
        functools.partial(ns_kernel, n, ax),
        name="newton_schulz",
        out_shape=outs,
        in_specs=[hbm] * 3 + [vmem] * 3,
        out_specs=[vmem] * 6,
        scratch_shapes=[
            pltpu.VMEM((2, n, n), BF16),
            pltpu.VMEM((n, n), BF16),
            pltpu.VMEM((n // 2, n), BF16),
            pltpu.VMEM((2, blk, blk), BF16),
            pltpu.VMEM((4 * max(wa.shape[0], wu.shape[0]), n), BF16),
            pltpu.VMEM(wa.shape, BF16),
            pltpu.VMEM(wu.shape, BF16),
            pltpu.VMEM(wd.shape, BF16),
            dma((4,)), dma((8,)), dma((8,)), dma((2,)), dma((2,)), dma((2, 4)), dma((2, 4)), dma((4,)), dma((3,)),
        ],
        compiler_params=pltpu.CompilerParams(collective_id=1, has_side_effects=True, vmem_limit_bytes=VMEM_LIMIT),
    )(xa, xu, xd, wa, wu, wd)


def solution(mesh):
    ax = mesh.axis_names[1]
    group = mesh.shape[ax]
    grad_spec = P(tuple(mesh.axis_names), None, None, None)
    row_spec = P(mesh.axis_names[0], ax, None)

    def step_local(*arrays):
        moms, gathered, masters = [], [], []
        for k in range(3):
            grad, mom, master = arrays[3 * k:3 * k + 3]
            grad_rows = lax.psum_scatter(grad[0, 0], ax, scatter_dimension=0, tiled=True) / group
            mom_new = MOMENTUM * mom[0] + grad_rows
            norm_sq = lax.psum(jnp.sum(mom_new * mom_new), ax)
            x_rows = (mom_new / (jnp.sqrt(norm_sq) + EPSILON)).astype(BF16)
            moms.append(mom_new)
            gathered.append(lax.all_gather(x_rows, ax, axis=0, tiled=True))
            masters.append(master[0])
        new = orthogonalize(ax, *gathered, *masters)
        results = []
        for k in range(3):
            results += [moms[k][None], new[2 * k][None], new[2 * k + 1][None]]
        return tuple(results)

    return jax.shard_map(step_local, mesh=mesh, in_specs=(grad_spec, row_spec, row_spec) * 3,
                         out_specs=(row_spec,) * 9, check_vma=False)
```

time: 1340 us -> 619 us (0.46); the launches traced: 1320 us -> 619 us
  starting transfers between devices: 362 us -> 0.37 us
  local copies, waits for them, and re-layouts: 193 us -> 10 us
  Pallas kernels: 0 us -> 122 us
  other arithmetic: 112 us -> 10.5 us
  matrix products: 98.5 us -> 0 us
  waiting for transfers between devices: 488 us -> 413 us
    all_to_all x6 -> x0, starting transfers between devices: 361 us -> none  [the longest x3 339 us: stack_step(): lax.all_to_all(ortho_mat.reshape(slots, 1, n_rows, n_cols), 'data', 2, 1,...]
    all_to_all x6 -> x0, waiting for transfers between devices: 202 us -> none  [the longest x3 150 us: stack_step(): lax.all_to_all(send_buf, 'data', 1, 2, tiled=True)]
    all_gather x0 -> x3, waiting for transfers between devices: none -> 126 us  [step_local(): gathered.append(lax.all_gather(x_rows, ax, axis=0, tiled=True))]
    pallas_call x0 -> x1, Pallas kernels: none -> 122 us  [orthogonalize(): pl.pallas_call(functools.partial(ns_kernel, n, ax), name='newton_schulz',...]
    unnamed x28 -> x12, local copies, waits for them, and re-layouts: 126 us -> 10 us
    unnamed x3 -> x0, other arithmetic: 104 us -> none
    dot_general x10 -> x0, matrix products: 98.5 us -> none  [the longest x5 58.5 us: newton_schulz(): jnp.einsum('bkc,brc->bkr', x_mat, poly_mat, preferred_element_type=jnp.fl...]
    reshape x7 -> x0, local copies, waits for them, and re-layouts: 60.5 us -> none  [the longest x3 44.8 us: stack_step(): ortho_mat.reshape(slots, 1, n_rows, n_cols)]
  transfers between devices with their start and end apart: 9 -> 6, of which waited for: 7 -> 6; matrix products, arithmetic and copies ran while one was open for 27% -> 1% of each run, Pallas kernels for 0% -> 0%
where the time goes in v1:
time: 619 us
  waiting for transfers between devices  413 us (67%)
  Pallas kernels  122 us (20%)
  blocking collectives  46.3 us (7%)
  between operations  16.3 us (3%)
  other arithmetic  10.5 us (2%)
  local copies, waits for them, and re-layouts  10 us (2%)
    reduce_scatter x3, waiting for transfers between devices, step_local(): lax.psum_scatter(grad[0, 0], ax, scatter_dimension=0, tiled=True) / group  285 us
    all_gather x3, waiting for transfers between devices, step_local(): gathered.append(lax.all_gather(x_rows, ax, axis=0, tiled=True))  126 us
    pallas_call x1, Pallas kernels, orthogonalize(): pl.pallas_call(functools.partial(ns_kernel, n, ax), name='newton_schulz',...  122 us
    psum x1, blocking collectives, step_local(): norm_sq = lax.psum(jnp.sum(mom_new * mom_new), ax)  46.3 us
  transfers between devices with their start and end apart: 6, of which 6 were waited for; matrix products, arithmetic and copies ran while one was open for 1% of the time, Pallas kernels for 0%

profile of v1, /device:TPU:97, one launch (start us, length us, event | category | flops | bytes accessed | tf_op | source)
XLA Modules:
  0.0 618.6 jit_solution(14281472621574466096)
XLA Ops:
  7.2 0.1 reduce-scatter.6.cloned.1.call-start
  7.3 0.7 reduce-scatter.6.cloned.1.call-update
  8.0 0.1 reduce-scatter.8.cloned.1.call-start
  8.1 0.7 reduce-scatter.8.cloned.1.call-update
  8.8 0.1 reduce-scatter.4.cloned.1.call-start
  8.9 0.0 copy-start.1
  8.9 0.0 copy-start.2
  8.9 0.0 copy-start
  8.9 0.7 reduce-scatter.4.cloned.1.call-update
  9.6 0.1 all-gather.6.cloned.1.call-start
  9.7 89.1 %reduce-scatter.6.cloned.1.call-done = f32[64,1024]{1,0:T(8,128)} async-done(((f32[2048,1024]{1,0:T(8,128)}), f32[64,1024]{1,0:T(8,128)}) %reduce-scatter.6.cloned.1.call-update) | async-done | bytes 262160 | tf_op jit(solution)/shard_map/reduce_scatter | solution.py:376
  98.7 0.0 copy-done.1
  98.7 1.6 multiply_reduce_fusion.2
  100.4 86.3 %reduce-scatter.8.cloned.1.call-done = f32[32,2048]{1,0:T(8,128)} async-done(((f32[1024,2048]{1,0:T(8,128)}), f32[32,2048]{1,0:T(8,128)}) %reduce-scatter.8.cloned.1.call-update) | async-done | bytes 262160 | tf_op jit(solution)/shard_map/reduce_scatter | solution.py:376
  186.7 0.0 copy-done.2
  186.7 1.6 multiply_reduce_fusion.1
  188.3 109.2 %reduce-scatter.4.cloned.1.call-done = f32[64,2048]{1,0:T(8,128)} async-done(((f32[2048,2048]{1,0:T(8,128)}), f32[64,2048]{1,0:T(8,128)}) %reduce-scatter.4.cloned.1.call-update) | async-done | bytes 524304 | tf_op jit(solution)/shard_map/reduce_scatter | solution.py:376
  297.5 0.0 copy-done
  297.5 1.8 multiply_reduce_fusion
  299.3 46.3 %all-reduce = (f32[]{:T(128)}, f32[]{:T(128)}, f32[]{:T(128)}) all-reduce(f32[]{:T(128)} %multiply_reduce_fusion, f32[]{:T(128)} %multiply_reduce_fusion.2, f32[]{:T(128)} %multiply_reduce_fusion.1), channel_id=1, replica_groups=mesh['stage'=1,'data'=32] {'data'}, use_global_device_ids=true, to_apply=%region_2.0 | all-reduce | flops 3 | bytes 24 | tf_op jit(solution)/shard_map/psum | solution.py:378
  346.3 1.7 fusion
  348.0 0.1 all-gather.6.cloned.1.call-update
  348.1 0.1 all-gather.8.cloned.1.call-start
  348.8 1.7 fusion.1
  350.6 0.1 all-gather.8.cloned.1.call-update
  350.6 0.1 all-gather.4.cloned.1.call-start
  351.4 2.0 divide_convert_fusion
  353.4 0.1 all-gather.4.cloned.1.call-update
  353.5 34.1 %all-gather.6.cloned.1.call-done.xu = bf16[2048,1024]{1,0:T(8,128)(2,1)} async-done(((bf16[64,1024]{1,0:T(8,128)(2,1)}), bf16[2048,1024]{1,0:T(8,128)(2,1)}) %all-gather.6.cloned.1.call-update) | async-done | bytes 4194320 | tf_op jit(solution)/shard_map/all_gather | solution.py:381
  387.5 42.8 %all-gather.8.cloned.1.call-done.xd = bf16[1024,2048]{1,0:T(8,128)(2,1)} async-done(((bf16[32,2048]{1,0:T(8,128)(2,1)}), bf16[1024,2048]{1,0:T(8,128)(2,1)}) %all-gather.8.cloned.1.call-update) | async-done | bytes 4194320 | tf_op jit(solution)/shard_map/all_gather | solution.py:381
  430.3 49.2 %all-gather.4.cloned.1.call-done.xa = bf16[2048,2048]{1,0:T(8,128)(2,1)} async-done(((bf16[64,2048]{1,0:T(8,128)(2,1)}), bf16[2048,2048]{1,0:T(8,128)(2,1)}) %all-gather.4.cloned.1.call-update) | async-done | bytes 8388624 | tf_op jit(solution)/shard_map/all_gather | solution.py:381
  479.5 122.2 %newton_schulz.1 = (f32[64,2048]{1,0:T(8,128)}, bf16[64,2048]{1,0:T(8,128)(2,1)}, f32[64,1024]{1,0:T(8,128)}, bf16[64,1024]{1,0:T(8,128)(2,1)}, f32[32,2048]{1,0:T(8,128)}, /*index=5*/bf16[32,2048]{1,0:T(8,128)(2,1)}) custom-call(bf16[2048,2048]{1,0:T(8,128)(2,1)} %all-gather.4.cloned.1.call-done.xa, bf16[2048,1024]{1,0:T(8,128)(2,1)} %all-gather.6.cloned.1.call-done.xu, ...), custom_call_target="tpu_custom_call" | custom-call | tf_op jit(solution)/shard_map/newton_schulz/pallas_call | solution.py:345
  601.7 1.9 copy.24
  603.6 1.7 copy.25
  605.2 1.7 copy.26
  606.9 1.6 copy.27
  608.5 1.7 copy.28
  610.1 1.6 copy.29
Async XLA Ops:
  7.2 91.5 %reduce-scatter.6.cloned.1.call-start = ((), (), s32[]{:S(2)}) async-start(), calls=%async_computation.5 | async-start | bytes 8650752 | tf_op jit(solution)/shard_map/reduce_scatter | solution.py:376
  8.0 178.7 %reduce-scatter.8.cloned.1.call-start = ((), (), s32[]{:S(2)}) async-start(), calls=%async_computation.7 | async-start | bytes 8650752 | tf_op jit(solution)/shard_map/reduce_scatter | solution.py:376
  8.8 288.7 %reduce-scatter.4.cloned.1.call-start = ((), (), s32[]{:S(2)}) async-start(), calls=%async_computation.3 | async-start | bytes 17301504 | tf_op jit(solution)/shard_map/reduce_scatter | solution.py:376
  8.9 89.9 %copy-start.1 = (f32[1,64,1024]{2,1,0:T(8,128)S(1)}, f32[1,64,1024]{2,1,0:T(8,128)}, u32[]{:S(2)}) copy-start(f32[1,64,1024]{2,1,0:T(8,128)} %param.13) | copy-start | bytes 786436
  8.9 177.8 %copy-start.2 = (f32[1,32,2048]{2,1,0:T(8,128)S(1)}, f32[1,32,2048]{2,1,0:T(8,128)}, u32[]{:S(2)}) copy-start(f32[1,32,2048]{2,1,0:T(8,128)} %param.16) | copy-start | bytes 786436
  8.9 288.6 %copy-start = (f32[1,64,2048]{2,1,0:T(8,128)S(1)}, f32[1,64,2048]{2,1,0:T(8,128)}, u32[]{:S(2)}) copy-start(f32[1,64,2048]{2,1,0:T(8,128)} %param.10) | copy-start | bytes 1572868
  9.6 378.0 %all-gather.6.cloned.1.call-start = ((), (), s32[]{:S(2)}) async-start(), calls=%async_computation.6 | async-start | bytes 4325376 | tf_op jit(solution)/shard_map/all_gather | solution.py:381
  348.1 82.2 %all-gather.8.cloned.1.call-start = ((), (), s32[]{:S(2)}) async-start(), calls=%async_computation.8 | async-start | bytes 4325376 | tf_op jit(solution)/shard_map/all_gather | solution.py:381
  350.6 128.9 %all-gather.4.cloned.1.call-start = ((), (), s32[]{:S(2)}) async-start(), calls=%async_computation.4 | async-start | bytes 8650752 | tf_op jit(solution)/shard_map/all_gather | solution.py:381
Sparse Core Ops, SparseCore 0:
  11.6 87.1 reduce-scatter.5
  102.3 84.3 reduce-scatter.7
  190.5 106.9 reduce-scatter.3
  348.2 39.3 all-gather.5
  390.0 40.1 all-gather.7
  432.8 46.6 all-gather.3

commit v2 on v1

v2 whole, which is shorter than its diff:
```python
import functools
import math

import jax
import jax.numpy as jnp
from jax import lax
from jax.experimental import pallas as pl
from jax.experimental.pallas import tpu as pltpu
from jax.sharding import PartitionSpec as P

MOMENTUM = 0.95
LEARN_RATE = 0.25
WEIGHT_DECAY = 0.2
EPSILON = 1e-7
COEF_A = 3.4445
COEF_B = -4.7750
COEF_C = 2.0315
NS_STEPS = 5
F32 = jnp.float32
BF16 = jnp.bfloat16
MESH = pl.DeviceIdType.MESH
VMEM_LIMIT = 66_000_000
ATTN, UP, DOWN = MATRICES = range(3)
FIRST, SECOND = PAIR = range(2)
ALL = slice(None)
QUAD = range(4)


class Comm:
    def __init__(self, side, group, ax, mats, slots, local_sem, send_sem, recv_sem):
        self.side, self.group, self.ax, self.mats, self.slots = side, group, ax, mats, slots
        self.local_sem, self.send_sem, self.recv_sem = local_sem, send_sem, recv_sem
        me = lax.axis_index(ax)
        self.role = lax.rem(me, 4)
        self.c = lax.rem(me, 2)
        self.x = lax.rem(me // 2, side)
        self.y = me // (2 * side)
        self.peer = self.dev(self.y, self.x, 1 - self.c)
        self.pos = ((self.x, self.y), (self.y, self.x))
        self.keys, self.local_keys, self.sent, self.peer_only = {}, {}, {}, {}

    def dev(self, yy, xx, cc):
        return {self.ax: (lax.rem(yy, self.side) * self.side + lax.rem(xx, self.side)) * 2 + cc}

    def greet(self):
        barrier = pltpu.get_barrier_semaphore()
        pl.semaphore_signal(barrier, inc=1, device_id=self.peer, device_id_type=MESH)
        for k in range(1, self.side):
            pl.semaphore_signal(barrier, inc=1, device_id=self.dev(self.y + k, self.x, self.c), device_id_type=MESH)
            pl.semaphore_signal(barrier, inc=1, device_id=self.dev(self.y, self.x + k, self.c), device_id_type=MESH)
        return 2 * self.side - 1

    def to(self, along_x, step):
        step = step % self.side
        return self.dev(self.y, self.x + step, self.c) if along_x else self.dev(self.y + step, self.x, self.c)

    def remote(self, key, src, dst, target):
        k = self.keys.setdefault(key, len(self.keys))
        return pltpu.make_async_remote_copy(src, dst, self.send_sem.at[k], self.recv_sem.at[k],
                                            device_id=target, device_id_type=MESH)

    def local(self, key, src, dst):
        k = self.local_keys.setdefault(key, len(self.local_keys))
        return pltpu.make_async_copy(src, dst, self.local_sem.at[k])

    def start(self, make, *args):
        make(*args).start()
        self.sent[(make.__name__,) + args] = (make, args)

    def finish(self):
        for make, args in self.sent.values():
            make(*args).wait_send()

    def shift(self, p, k):
        return lax.rem(p + k, self.side)

    def quarter(self, m, f, h):
        q = self.mats[m]["own"].shape[-1] // 4
        return pl.ds((2 * f + h) * q, q)

    def half(self, m, f):
        q = self.mats[m]["own"].shape[-1] // 2
        return pl.ds(f * q, q)

    @staticmethod
    def lane1(f, k):
        return (ALL, k) if f == 0 else (k, ALL)

    def lane2(self, f, k):
        return (k, self.x) if f == 0 else (self.y, k)

    @staticmethod
    def one(f, k, i):
        return (i, k) if f == 0 else (k, i)

    def pair_remote(self, m, f, k):
        idx = self.lane1(f, self.shift(self.pos[f][0], k))
        cols = self.half(m, f)
        mat = self.mats[m]
        return self.remote(("pair", m, f, k), mat["grad"].at[idx + (1 - self.c, ALL, cols)],
                           mat["peer"].at[idx + (ALL, cols)], self.peer)

    def pair_local(self, m, f, k):
        idx = self.lane1(f, self.shift(self.pos[f][0], k))
        cols = self.half(m, f)
        mat = self.mats[m]
        return self.local(("pair", m, f, k), mat["grad"].at[idx + (self.c, ALL, cols)],
                          mat["sum"].at[idx + (ALL, cols)])

    def pair_start(self, m):
        for k in (2, 1, self.side - 1, 0):
            for f in PAIR:
                self.start(self.pair_remote, m, f, k)
                self.pair_local(m, f, k).start()

    def pair_sum(self, m, f, k):
        self.pair_remote(m, f, k).wait_recv()
        self.pair_local(m, f, k).wait()
        kk = self.shift(self.pos[f][0], k)
        cols = self.half(m, f)
        total, other = self.mats[m]["sum"], self.mats[m]["peer"]

        @pl.loop(0, self.side)
        def _(i):
            idx = self.one(f, kk, i) + (ALL, cols)
            total[idx] = total[idx] + other[idx]

    def ring(self, m, f, phase, j):
        k, h, step = ((2, 1, 1), (2, 0, -1), (1, 0, 1), (-1, 1, -1), (1, 1, 1), (-1, 0, -1))[j]
        kk = self.shift(self.pos[f][phase], k % self.side)
        idx = (self.lane1, self.lane2)[phase](f, kk) + (ALL, self.quarter(m, f, h))
        mat = self.mats[m]
        return self.remote(("ring", m, f, phase, j), mat["sum"].at[idx], mat[("ring1", "ring2")[phase]].at[f, j],
                           self.to((f == 0) == (phase == 0), step))

    def ring_add(self, m, f, phase, j, k, h):
        self.ring(m, f, phase, j).wait_recv()
        kk = self.shift(self.pos[f][phase], k % self.side)
        cols = self.quarter(m, f, h)
        mat = self.mats[m]
        total = mat["sum"]
        if phase == 0:
            @pl.loop(0, self.side)
            def _(i):
                idx = self.one(f, kk, i) + (ALL, cols)
                total[idx] = total[idx] + mat["ring1"][f, j, i]
        else:
            idx = self.lane2(f, kk) + (ALL, cols)
            total[idx] = total[idx] + mat["ring2"][f, j]

    def rs_far(self, m):
        for f in PAIR:
            self.pair_sum(m, f, 2)
            self.start(self.ring, m, f, 0, 0)
            self.start(self.ring, m, f, 0, 1)

    def rs_near(self, m):
        for f in PAIR:
            self.pair_sum(m, f, 1)
            self.start(self.ring, m, f, 0, 2)
            self.pair_sum(m, f, self.side - 1)
            self.start(self.ring, m, f, 0, 3)

    def rs_own(self, m):
        for f in PAIR:
            self.pair_sum(m, f, 0)

    def pass_on(self, m, phase):
        for f in PAIR:
            self.ring_add(m, f, phase, 0, 1, 1)
            self.start(self.ring, m, f, phase, 4)
            self.ring_add(m, f, phase, 1, -1, 0)
            self.start(self.ring, m, f, phase, 5)

    def settle(self, m, phase):
        for f in PAIR:
            for j, h in ((2, 0), (3, 1), (4, 1), (5, 0)):
                self.ring_add(m, f, phase, j, 0, h)
            if phase == 0:
                for j in range(4):
                    self.start(self.ring, m, f, 1, j)

    def norm_pair(self, m):
        ref = self.slots.at[m, 0, self.c]
        return self.remote(("norm", m), ref, ref, self.peer)

    def norm_line(self, m, level, k):
        ref = self.slots.at[m, level, self.x if level == 1 else self.y]
        return self.remote(("norm", m, level, k), ref, ref, self.to(level == 1, k))

    def momentum(self, m):
        mat = self.mats[m]
        rows, cols = mat["mom"].shape
        mat["new"][...] = MOMENTUM * mat["mom"][...] + mat["sum"][self.y, self.x] / self.group
        acc = jnp.zeros((8, 128), F32)
        for i in range(0, rows, 8):
            for j in range(0, cols, 128):
                part = mat["new"][i:i + 8, j:j + 128]
                acc = acc + part * part
        self.slots[m, 0, self.c] = acc
        self.start(self.norm_pair, m)

    def norm_x(self, m):
        self.norm_pair(m).wait_recv()
        self.slots[m, 1, self.x] = self.slots[m, 0, 0] + self.slots[m, 0, 1]
        for k in range(1, self.side):
            self.start(self.norm_line, m, 1, k)

    def level_sum(self, m, level):
        for k in range(1, self.side):
            self.norm_line(m, level, k).wait_recv()
        acc = self.slots[m, level, 0]
        for k in range(1, self.side):
            acc = acc + self.slots[m, level, k]
        return acc

    def norm_y(self, m):
        self.slots[m, 2, self.y] = self.level_sum(m, 1)
        for k in range(1, self.side):
            self.start(self.norm_line, m, 2, k)

    def normalize(self, m):
        mat = self.mats[m]
        norm = jnp.sqrt(jnp.sum(self.level_sum(m, 2), axis=(0, 1), keepdims=True))
        mat["own"][...] = (mat["new"][...] / (norm + EPSILON)).astype(BF16)

    def along(self, f, phase):
        return (f == 0) != (phase == 0)

    def gpos(self, f, phase):
        return self.x if self.along(f, phase) else self.y

    def spot(self, m, f, phase, k, cols):
        if phase == 0:
            idx = (k, self.x) if f == 0 else (self.y, k)
        else:
            idx = self.lane1(f, k)
        return self.mats[m]["full"].at[idx + (self.c, ALL, cols)]

    def ag_own(self, m):
        return self.local(("own", m), self.mats[m]["own"], self.mats[m]["full"].at[self.y, self.x, self.c])

    def ag_send(self, m, f, phase, j):
        dst = self.spot(m, f, phase, self.gpos(f, phase), self.half(m, f))
        src = self.mats[m]["own"].at[:, self.half(m, f)] if phase == 0 else dst
        return self.remote(("send", m, f, phase, j), src, dst, self.to(self.along(f, phase), (1, -1)[j]))

    def ag_relay(self, m, f, phase, j):
        ref = self.spot(m, f, phase, self.shift(self.gpos(f, phase), (self.side - 1, 1)[j]), self.quarter(m, f, (1, 0)[j]))
        return self.remote(("relay", m, f, phase, j), ref, ref, self.to(self.along(f, phase), (1, -1)[j]))

    def ag_peer(self, m, f, k):
        ref = self.spot(m, f, 1, self.shift(self.gpos(f, 1), k), self.half(m, f))
        return self.remote(("peer", m, f, k), ref, ref, self.peer)

    def to_peer(self, m, f, k):
        self.peer_only[m, f, k] = True

        @pl.when(self.sends(m))
        def _():
            self.ag_peer(m, f, k).start()

    def sends(self, m):
        return self.role < 2 if m == 0 else self.role == 4 - m

    def needs(self, m):
        return self.role < 2 if m == 0 else self.role == 1 + m

    def ag_start(self, m):
        self.ag_own(m).start()
        for f in PAIR:
            for j in PAIR:
                self.start(self.ag_send, m, f, 0, j)

    def ag_forward(self, m, phase):
        for f in PAIR:
            for j in PAIR:
                self.ag_send(m, f, phase, j).wait_recv()
                self.start(self.ag_relay, m, f, phase, j)
                if phase == 1:
                    self.to_peer(m, f, (self.side - 1, 1)[j])

    def ag_turn(self, m):
        self.ag_own(m).wait()
        for f in PAIR:
            for j in PAIR:
                self.ag_relay(m, f, 0, j).wait_recv()
            for j in PAIR:
                self.start(self.ag_send, m, f, 1, j)
            self.to_peer(m, f, 0)

    def ag_end(self, m):
        for f in PAIR:
            for j in PAIR:
                self.ag_relay(m, f, 1, j).wait_recv()
            self.to_peer(m, f, 2)

    def ag_arrived(self, m):
        @pl.when(self.needs(m))
        def _():
            for f in PAIR:
                for k in range(self.side):
                    self.ag_peer(m, f, k).wait_recv()

    def ag_finish(self, m):
        @pl.when(self.sends(m))
        def _():
            for f in PAIR:
                for k in range(self.side):
                    self.ag_peer(m, f, k).wait_send()


def reduce_kernel(side, group, ax, ga, gu, ma, mu, na, nu, xu, xa,
                  sa, su, pa, pu, ra1, ru1, ra2, ru2, xra, slots, local_sem, send_sem, recv_sem):
    mats = {0: dict(grad=ga, mom=ma, new=na, full=xa, sum=sa, peer=pa, ring1=ra1, ring2=ra2, own=xra),
            1: dict(grad=gu, mom=mu, new=nu, sum=su, peer=pu, ring1=ru1, ring2=ru2, own=xu)}
    comm = Comm(side, group, ax, mats, slots, local_sem, send_sem, recv_sem)
    pl.semaphore_wait(pltpu.get_barrier_semaphore(), comm.greet())
    comm.pair_start(ATTN)
    comm.pair_start(UP)
    comm.rs_far(ATTN)
    comm.rs_near(ATTN)
    comm.rs_own(ATTN)
    comm.pass_on(ATTN, FIRST)
    comm.settle(ATTN, FIRST)
    comm.pass_on(ATTN, SECOND)
    comm.rs_far(UP)
    comm.settle(ATTN, SECOND)
    comm.momentum(ATTN)
    comm.rs_near(UP)
    comm.norm_x(ATTN)
    comm.rs_own(UP)
    comm.norm_y(ATTN)
    comm.normalize(ATTN)
    comm.ag_start(ATTN)
    comm.pass_on(UP, FIRST)
    comm.ag_forward(ATTN, FIRST)
    comm.ag_turn(ATTN)
    comm.settle(UP, FIRST)
    comm.pass_on(UP, SECOND)
    comm.ag_forward(ATTN, SECOND)
    comm.settle(UP, SECOND)
    comm.momentum(UP)
    comm.norm_x(UP)
    comm.norm_y(UP)
    comm.normalize(UP)
    comm.ag_end(ATTN)
    comm.ag_arrived(ATTN)
    comm.finish()
    comm.ag_finish(ATTN)


def scratch_for(side, shapes):
    scratch = [pltpu.VMEM((side, side) + s, F32) for s in shapes] * 2
    scratch += [pltpu.VMEM((2, 6, side, s[0], s[1] // 4), F32) for s in shapes]
    scratch += [pltpu.VMEM((2, 6, s[0], s[1] // 4), F32) for s in shapes]
    return scratch


def reduce_and_gather(side, ax, grads, moms):
    dma = pltpu.SemaphoreType.DMA
    vmem = pl.BlockSpec(memory_space=pltpu.VMEM)
    hbm = pl.BlockSpec(memory_space=pl.ANY)
    group = 2 * side * side
    shapes = [m.shape for m in moms]
    views = [g.reshape(side, side, 2, *s) for g, s in zip(grads, shapes)]
    scratch = scratch_for(side, shapes) + [pltpu.VMEM(shapes[0], BF16)]
    scratch += [pltpu.VMEM((2, 3, side, 8, 128), F32), dma((20,)), dma((110,)), dma((110,))]
    na, nu, xu, xa = pl.pallas_call(
        functools.partial(reduce_kernel, side, group, ax),
        name="reduce_gather",
        out_shape=[jax.ShapeDtypeStruct(s, F32) for s in shapes]
        + [jax.ShapeDtypeStruct(shapes[1], BF16), jax.ShapeDtypeStruct((side, side, 2) + shapes[0], BF16)],
        in_specs=[hbm] * 2 + [vmem] * 2,
        out_specs=[vmem] * 3 + [hbm],
        scratch_shapes=scratch,
        compiler_params=pltpu.CompilerParams(collective_id=0, has_side_effects=True, vmem_limit_bytes=VMEM_LIMIT),
    )(*views, *moms)
    return na, nu, xu, xa.reshape(group * shapes[0][0], shapes[0][1])


def ns_kernel(n, side, group, ax, xa, xur, gd, md, oa_out, ou_out, od_out, nd, xu, xd,
              X, A, B, stage, obuf, oa, ou, od, sd, pd, rd1, rd2, xrd, slots,
              load_sem, asend, arecv, bsend, brecv, xsend, xrecv, osend, orecv, local_sem, send_sem, recv_sem):
    me = lax.axis_index(ax)
    role = lax.rem(me, 4)
    base = me - role
    mats = {1: dict(full=xu, own=xur),
            2: dict(grad=gd, mom=md, new=nd, full=xd, sum=sd, peer=pd, ring1=rd1, ring2=rd2, own=xrd)}
    comm = Comm(side, group, ax, mats, slots, local_sem, send_sem, recv_sem)
    blk = n // 4
    half = n // 2

    def dev(k):
        return {ax: k}

    barrier = pltpu.get_barrier_semaphore()
    greeted = comm.greet()
    for step in range(1, 4):
        pl.semaphore_signal(barrier, inc=1, device_id=dev(base + lax.rem(role + step, 4)), device_id_type=MESH)
    pl.semaphore_wait(barrier, greeted + 3)
    comm.pair_start(DOWN)
    comm.ag_start(UP)
    steps = (
        ("0A1", (comm.rs_far, DOWN)),
        ("0A2", (comm.rs_near, DOWN)),
        ("0A4", (comm.ag_forward, UP, FIRST)),
        ("0Q1", (comm.rs_own, DOWN), (comm.pass_on, DOWN, FIRST)),
        ("0Q3", (comm.ag_turn, UP)),
        ("0P2", (comm.settle, DOWN, FIRST)),
        ("0S1", (comm.pass_on, DOWN, SECOND)),
        ("1A0", (comm.settle, DOWN, SECOND), (comm.momentum, DOWN)),
        ("1A1", (comm.norm_x, DOWN)),
        ("1A3", (comm.norm_y, DOWN)),
        ("1Q0", (comm.normalize, DOWN), (comm.ag_start, DOWN)),
        ("1Q1", (comm.ag_forward, UP, SECOND)),
        ("1Q3", (comm.ag_forward, DOWN, FIRST)),
        ("1P1", (comm.ag_turn, DOWN)),
        ("1P3", (comm.ag_end, UP)),
        ("1S3", (comm.ag_forward, DOWN, SECOND)),
        ("2A2", (comm.ag_end, DOWN)),
    )

    def run(calls):
        for call, *what in calls:
            call(*what)

    def tick(t, part, i):
        if isinstance(t, int):
            return
        for (when, where, block), *calls in steps:
            if where == part:
                go = jnp.logical_and(t == int(when), i == int(block))
                pl.when(go)(functools.partial(run, calls))

    def at(ref, i, j):
        return ref.at[pl.ds(pl.multiple_of(i * blk, blk), blk), pl.ds(pl.multiple_of(j * blk, blk), blk)]

    def rows(i, size=blk):
        return pl.ds(pl.multiple_of(i * size, size), size)

    def poly(a, q):
        return (COEF_B * a.astype(F32) + COEF_C * q.astype(BF16).astype(F32)).astype(BF16)

    def blend(x, y):
        return (COEF_A * x.astype(F32) + y.astype(BF16).astype(F32)).astype(BF16)

    def dot_nt(a, b):
        return lax.dot_general(a, b, (((1,), (1,)), ((), ())), preferred_element_type=F32)

    def dot(a, b):
        return jnp.dot(a, b, preferred_element_type=F32)

    @pl.when(role < 2)
    def _():
        c = role
        peer = dev(base + 1 - c)
        p_own, s_own = 3 * c, 1 + c
        p_peer, s_peer = 3 - 3 * c, 2 - c
        i1, j1 = 1 + 2 * c, 3 - 3 * c
        i2, j2 = 2 * c, 2 - c

        loads = [pltpu.make_async_copy(xa.at[rows(p)], X.at[0, rows(p)], load_sem.at[k])
                 for k, p in enumerate((p_own, s_own, p_peer, s_peer))]
        for cp in loads:
            cp.start()
        for cp in loads:
            cp.wait()

        def a_copy(k, i, j):
            return pltpu.make_async_remote_copy(at(A, i, j), at(A, i, j), asend.at[k], arecv.at[k],
                                                device_id=peer, device_id_type=MESH)

        a_blocks = ((p_own, p_own), (p_own, s_own), (s_own, p_own), (i1, j1), (j1, i1), (i2, j2), (j2, i2), (s_own, s_own))
        PP, PS, SP, C1, T1, C2, T2, SS = every = range(len(a_blocks))

        def a_send(k):
            a_copy(k, *a_blocks[k]).start()

        def a_wait(*ks):
            for k in ks:
                a_copy(k, *a_blocks[k]).wait_recv()

        def x_copy(nxt, p, j, k):
            ref = at(X.at[nxt], p, j)
            return pltpu.make_async_remote_copy(ref, ref, xsend.at[k, j], xrecv.at[k, j],
                                                device_id=peer, device_id_type=MESH)

        def x_wait(cur, k):
            for j in QUAD:
                x_copy(cur, (p_peer, s_peer)[k], j, k).wait_recv()

        def b_copy(k):
            i, j = ((i1, j1), (i2, j2))[k]
            return pltpu.make_async_remote_copy(stage.at[k], at(B, j - 2 * (1 - c), i), bsend.at[k], brecv.at[k],
                                                device_id=peer, device_id_type=MESH)

        def gram(xt, i, j, mirror):
            v = dot_nt(xt[rows(i), :], xt[rows(j), :]).astype(BF16)
            at(A, i, j)[...] = v
            if mirror:
                at(A, j, i)[...] = v.T

        def a_step(t, cur):
            xt = X.at[cur]
            gram(xt, p_own, p_own, False)
            tick(t, "A", 0)

            @pl.when(t > 0)
            def _():
                x_wait(cur, FIRST)
            a_send(PP)
            gram(xt, p_own, s_own, True)
            a_send(PS)
            a_send(SP)
            tick(t, "A", 1)
            gram(xt, i1, j1, True)
            a_send(C1)
            a_send(T1)
            tick(t, "A", 2)

            @pl.when(t > 0)
            def _():
                x_wait(cur, SECOND)
            gram(xt, i2, j2, True)
            a_send(C2)
            a_send(T2)
            tick(t, "A", 3)
            gram(xt, s_own, s_own, False)
            a_send(SS)
            tick(t, "A", 4)

        def x_wait_send(nxt):
            for k, p in enumerate((p_own, s_own)):
                for j in QUAD:
                    x_copy(nxt, p, j, k).wait_send()

        def q_block(i, j):
            q = dot(A[rows(i), :], A[:, pl.ds(pl.multiple_of(j * blk, blk), blk)])
            v = poly(at(A, i, j)[...], q)
            at(B, i - 2 * c, j)[...] = v
            return v

        def q_step(t, cur):
            a_wait(C1, T1)
            q_block(p_own, p_own)
            tick(t, "Q", 0)
            a_wait(C2, T2)
            v = q_block(p_own, s_own)
            at(B, s_own - 2 * c, p_own)[...] = v.T
            tick(t, "Q", 1)
            a_wait(PP, PS, SP)
            v = q_block(i1, j1)
            stage[FIRST] = v.T
            b_copy(FIRST).start()
            tick(t, "Q", 2)
            a_wait(SS)
            v = q_block(i2, j2)
            stage[SECOND] = v.T
            b_copy(SECOND).start()
            tick(t, "Q", 3)
            q_block(s_own, s_own)
            tick(t, "Q", 4)
            for k in every:
                a_copy(k, *a_blocks[k]).wait_send()

            @pl.when(t > 0)
            def _():
                x_wait_send(cur)

        def y_step(t, cur, nxt):
            xt, xn = X.at[cur], X.at[nxt]
            for k, p in enumerate((p_own, s_own)):
                b_copy(k).wait_recv()

                @pl.loop(0, 4)
                def _(j):
                    cols = pl.ds(pl.multiple_of(j * blk, blk), blk)
                    y = dot(B[rows(p - 2 * c), :], xt[:, cols])
                    at(xn, p, j)[...] = blend(at(xt, p, j)[...], y)
                    x_copy(nxt, p, j, k).start()
                    tick(t, "PS"[k], j)
            for k in PAIR:
                b_copy(k).wait_send()

        @pl.loop(0, NS_STEPS - 1)
        def _(t):
            cur = lax.rem(t, 2)
            nxt = 1 - cur
            a_step(t, cur)
            q_step(t, cur)
            y_step(t, cur, nxt)

        last = NS_STEPS - 1
        cur = last % 2
        a_step(last, cur)
        a_wait(*every)
        for k in every:
            a_copy(k, *a_blocks[k]).wait_send()
        x_wait_send(cur)
        own = oa.shape[0]
        mine = pl.ds(pl.multiple_of(own * (base + 2 * c), 2 * own), 2 * own)
        for j in QUAD:
            cols = pl.ds(j * blk, blk)
            B[0:2 * own, cols] = poly(A[mine, cols], dot(A[mine, :], A[:, cols]))
        for j in QUAD:
            cols = pl.ds(j * blk, blk)
            obuf[0:2 * own, cols] = blend(X[cur, mine, cols], dot(B[0:2 * own, :], X[cur, :, cols]))

        def o_copy(k, target):
            return pltpu.make_async_remote_copy(obuf.at[pl.ds(own * k, own)], oa, osend.at[k], orecv.at[0],
                                                device_id=dev(target), device_id_type=MESH)

        @pl.when(c == 1)
        def _():
            o_copy(0, base + 2).start()
            o_copy(1, base + 3).start()
            o_copy(0, base + 2).wait_send()
            o_copy(1, base + 3).wait_send()

        @pl.when(c == 0)
        def _():
            o_copy(1, base + 1).start()
            oa[...] = obuf[0:own, :]
            o_copy(1, base + 1).wait_send()

    @pl.when(role >= 2)
    def _():
        for _, *calls in steps:
            run(calls)
        comm.ag_arrived(UP)
        comm.ag_arrived(DOWN)

        def load(full, place):
            own = full.shape[3]
            copies = [pltpu.make_async_copy(full.at[yy, xx, cc], place(pl.ds(((yy * side + xx) * 2 + cc) * own, own)),
                                            load_sem.at[(yy * side + xx) * 2 + cc])
                      for yy in range(side) for xx in range(side) for cc in PAIR]
            for cp in copies:
                cp.start()
            for cp in copies:
                cp.wait()

        @pl.when(role == 2)
        def _():
            load(xu, lambda rows_at: X.at[1, rows_at, pl.ds(0, half)])

            @pl.loop(0, 4)
            def _(i):
                for j in PAIR:
                    at(X.at[0], j, i)[...] = at(X.at[1], i, j)[...].T

        @pl.when(role == 3)
        def _():
            load(xd, lambda rows_at: X.at[0, rows_at])

        pairs = ((0, 0), (0, 1), (1, 1))

        def a_step(cur):
            for i, j in pairs:
                v = dot_nt(X[cur, i * blk:(i + 1) * blk, :], X[cur, j * blk:(j + 1) * blk, :]).astype(BF16)
                at(A, i, j)[...] = v
                if i != j:
                    at(A, j, i)[...] = v.T

        def q_step():
            for i, j in pairs:
                v = poly(at(A, i, j)[...], dot(A[i * blk:(i + 1) * blk, 0:half], A[0:half, j * blk:(j + 1) * blk]))
                at(B, i, j)[...] = v
                if i != j:
                    at(B, j, i)[...] = v.T

        @pl.loop(0, NS_STEPS - 1)
        def _(t):
            cur = lax.rem(t, 2)
            nxt = 1 - cur
            a_step(cur)

            q_step()

            @pl.loop(0, 4)
            def _(j):
                cols = pl.ds(pl.multiple_of(j * blk, blk), blk)
                for i in PAIR:
                    y = dot(B[i * blk:(i + 1) * blk, 0:half], X[cur, 0:half, cols])
                    at(X.at[nxt], i, j)[...] = blend(at(X.at[cur], i, j)[...], y)

        cur = (NS_STEPS - 1) % 2
        a_step(cur)

        @pl.when(role == 2)
        def _():
            own = ou.shape[0]
            cols = pl.ds(pl.multiple_of(own * base, 4 * own), 4 * own)
            q_step()
            for i in PAIR:
                o = blend(X[cur, i * blk:(i + 1) * blk, cols], dot(B[i * blk:(i + 1) * blk, 0:half], X[cur, 0:half, cols]))
                obuf[0:4 * own, i * blk:(i + 1) * blk] = o.T

            def o_copy(k):
                return pltpu.make_async_remote_copy(obuf.at[pl.ds(own * k, own), pl.ds(0, half)], ou, osend.at[k], orecv.at[1],
                                                    device_id=dev(base + k), device_id_type=MESH)
            for k in (0, 1, 3):
                o_copy(k).start()
            ou[...] = obuf[2 * own:3 * own, 0:half]
            for k in (0, 1, 3):
                o_copy(k).wait_send()

        @pl.when(role == 3)
        def _():
            own = od.shape[0]
            mine = pl.ds(pl.multiple_of(own * base, 4 * own), 4 * own)
            for j in PAIR:
                cols = pl.ds(j * blk, blk)
                B[0:4 * own, cols] = poly(A[mine, cols], dot(A[mine, 0:half], A[0:half, cols]))
            for j in QUAD:
                cols = pl.ds(j * blk, blk)
                obuf[0:4 * own, cols] = blend(X[cur, mine, cols], dot(B[0:4 * own, 0:half], X[cur, 0:half, cols]))

            def o_copy(k):
                return pltpu.make_async_remote_copy(obuf.at[pl.ds(own * k, own)], od, osend.at[k], orecv.at[2],
                                                    device_id=dev(base + k), device_id_type=MESH)
            for k in (0, 1, 2):
                o_copy(k).start()
            od[...] = obuf[3 * own:4 * own, :]
            for k in (0, 1, 2):
                o_copy(k).wait_send()

    def arrived(o, k):
        pltpu.make_async_remote_copy(o, o, osend.at[k], orecv.at[k], device_id=dev(base), device_id_type=MESH).wait_recv()

    @pl.when(role != 3)
    def _():
        arrived(od, 2)
    od_out[...] = od[...]

    @pl.when(role != 2)
    def _():
        arrived(ou, 1)
    ou_out[...] = ou[...]

    @pl.when(role != 0)
    def _():
        arrived(oa, 0)
    oa_out[...] = oa[...]
    comm.finish()
    comm.ag_finish(UP)
    comm.ag_finish(DOWN)


def orthogonalize(side, ax, xa, xu, grad_down, mom_down):
    n = xa.shape[1]
    blk = n // 4
    group = 2 * side * side
    dma = pltpu.SemaphoreType.DMA
    vmem = pl.BlockSpec(memory_space=pltpu.VMEM)
    hbm = pl.BlockSpec(memory_space=pl.ANY)
    own_a, own_u, own_d = (n // group, n), xu.shape, mom_down.shape
    scratch = [
        pltpu.VMEM((2, n, n), BF16),
        pltpu.VMEM((n, n), BF16),
        pltpu.VMEM((n // 2, n), BF16),
        pltpu.VMEM((2, blk, blk), BF16),
        pltpu.VMEM((4 * max(own_a[0], own_u[0]), n), BF16),
        pltpu.VMEM(own_a, BF16),
        pltpu.VMEM(own_u, BF16),
        pltpu.VMEM(own_d, BF16),
    ]
    scratch += scratch_for(side, [own_d]) + [pltpu.VMEM(own_d, BF16), pltpu.VMEM((3, 3, side, 8, 128), F32)]
    scratch += [dma((group,)), dma((8,)), dma((8,)), dma((2,)), dma((2,)), dma((2, 4)), dma((2, 4)), dma((4,)), dma((3,))]
    scratch += [dma((20,)), dma((90,)), dma((90,))]
    oa, ou, od, nd, _, _ = pl.pallas_call(
        functools.partial(ns_kernel, n, side, group, ax),
        name="newton_schulz",
        out_shape=[jax.ShapeDtypeStruct(s, BF16) for s in (own_a, own_u, own_d)]
        + [jax.ShapeDtypeStruct(own_d, F32)]
        + [jax.ShapeDtypeStruct((side, side, 2) + s, BF16) for s in (own_u, own_d)],
        in_specs=[hbm, vmem, hbm, vmem],
        out_specs=[vmem] * 4 + [hbm] * 2,
        scratch_shapes=scratch,
        compiler_params=pltpu.CompilerParams(collective_id=1, has_side_effects=True, vmem_limit_bytes=VMEM_LIMIT),
    )(xa, xu, grad_down.reshape(side, side, 2, *own_d), mom_down)
    return oa, ou, od, nd


def update_kernel(scales, *refs):
    for k, scale in enumerate(scales):
        o, new, w = refs[3 * k:3 * k + 3]
        new_out, w_out, b_out = refs[9 + 3 * k:12 + 3 * k]
        new_out[...] = new[...]
        old = w[...]
        updated = old - LEARN_RATE * (scale * o[...].astype(F32) + WEIGHT_DECAY * old)
        w_out[...] = updated
        b_out[...] = updated.astype(BF16)


def update(group, orthos, moms, masters):
    args, outs, scales = [], [], []
    for o, new, w in zip(orthos, moms, masters):
        args += [o, new, w]
        outs += [jax.ShapeDtypeStruct(w.shape, F32)] * 2 + [jax.ShapeDtypeStruct(w.shape, BF16)]
        scales.append(0.2 * math.sqrt(max(group * w.shape[0], w.shape[1])))
    vmem = pl.BlockSpec(memory_space=pltpu.VMEM)
    return pl.pallas_call(
        functools.partial(update_kernel, scales), name="update", out_shape=outs,
        in_specs=[vmem] * 9, out_specs=[vmem] * 9,
    )(*args)


def solution(mesh):
    ax = mesh.axis_names[1]
    group = mesh.shape[ax]
    side = math.isqrt(group // 2)
    grad_spec = P(tuple(mesh.axis_names), None, None, None)
    row_spec = P(mesh.axis_names[0], ax, None)

    def step_local(*arrays):
        grads = [arrays[3 * k][0, 0] for k in range(3)]
        moms = [arrays[3 * k + 1][0] for k in range(3)]
        masters = [arrays[3 * k + 2][0] for k in range(3)]
        na, nu, xu, xa = reduce_and_gather(side, ax, grads[:2], moms[:2])
        oa, ou, od, nd = orthogonalize(side, ax, xa, xu, grads[2], moms[2])
        return tuple(r[None] for r in update(group, (oa, ou, od), (na, nu, nd), masters))

    return jax.shard_map(step_local, mesh=mesh, in_specs=(grad_spec, row_spec, row_spec) * 3,
                         out_specs=(row_spec,) * 9, check_vma=False)
```

time: 619 us -> 264 us (0.43)
  waiting for transfers between devices: 413 us -> 0 us
  Pallas kernels: 122 us -> 260 us
  blocking collectives: 46.3 us -> 0 us
  between operations: 16.3 us -> 1.1 us
  other arithmetic: 10.5 us -> 0 us
  local copies, waits for them, and re-layouts: 10 us -> 0 us
    reduce_scatter x3 -> x0, waiting for transfers between devices: 285 us -> none  [step_local(): lax.psum_scatter(grad[0, 0], ax, scatter_dimension=0, tiled=True) / group]
    pallas_call x1 -> x3, Pallas kernels: 122 us -> 260 us  [the longest x1 138 us: orthogonalize(): pl.pallas_call(functools.partial(ns_kernel, n, side, group, ax), name='ne...]
    all_gather x3 -> x0, waiting for transfers between devices: 126 us -> none  [step_local(): gathered.append(lax.all_gather(x_rows, ax, axis=0, tiled=True))]
    psum x1 -> x0, blocking collectives: 46.3 us -> none  [step_local(): norm_sq = lax.psum(jnp.sum(mom_new * mom_new), ax)]
    unnamed x12 -> x0, local copies, waits for them, and re-layouts: 10 us -> none
  transfers between devices with their start and end apart: 6 -> 0, of which waited for: 6 -> 0; matrix products, arithmetic and copies ran while one was open for 1% -> 0% of each run, Pallas kernels for 0% -> 0%
where the time goes in v2:
time: 264 us; the launch traced here: 261 us
  Pallas kernels  260 us (98%)
    pallas_call x1, Pallas kernels, orthogonalize(): pl.pallas_call(functools.partial(ns_kernel, n, side, group, ax), name='ne...  138 us
    pallas_call x1, Pallas kernels, reduce_and_gather(): pl.pallas_call(functools.partial(reduce_kernel, side, group, ax), name='r...  118 us

profile of v2, /device:TPU:97, one launch (start us, length us, event | category | flops | bytes accessed | tf_op | source)
XLA Modules:
  0.0 260.7 jit_solution(9726284564662766810)
XLA Ops:
  0.6 118.2 %reduce_gather.1 = (f32[64,2048]{1,0:T(8,128)}, f32[64,1024]{1,0:T(8,128)}, bf16[64,1024]{1,0:T(8,128)(2,1)}, bf16[4,4,2,64,2048]{4,3,2,1,0:T(8,128)(2,1)}) custom-call(f32[4,4,2,64,2048]{4,3,2,1,0:T(8,128)} %bitcast.19, f32[4,4,2,64,1024]{4,3,2,1,0:T(8,128)} %bitcast.20, f32[64,2048]{1,0:T(8,128)} %bitcast.23, f32[64,1024]{1,0:T(8,128)} %bitcast.25), custom_call_target="tpu_custom_call" | custom-call | tf_op jit(solution)/shard_map/reduce_gather/pallas_call | solution.py:369
  118.9 138.1 %newton_schulz.1 = (bf16[64,2048]{1,0:T(8,128)(2,1)}, bf16[64,1024]{1,0:T(8,128)(2,1)}, bf16[32,2048]{1,0:T(8,128)(2,1)}, f32[32,2048]{1,0:T(8,128)}, bf16[4,4,2...) custom-call(bf16[2048,2048]{1,0:T(8,128)(2,1)} %bitcast.22, bf16[64,1024]{1,0:T(8,128)(2,1)} %get-tuple-element.27.xur, ...), custom_call_target="tpu_custom_call" | custom-call | tf_op jit(solution)/shard_map/newton_schulz/pallas_call | solution.py:772
  257.0 3.3 %update.1 = (f32[64,2048]{1,0:T(8,128)}, f32[64,2048]{1,0:T(8,128)}, bf16[64,2048]{1,0:T(8,128)(2,1)}, f32[64,1024]{1,0:T(8,128)}, f32[64,1024]{1,0:T(8,128)}, /...) custom-call(bf16[64,2048]{1,0:T(8,128)(2,1)} %get-tuple-element.28.refs_0_, ...), custom_call_target="tpu_custom_call" | custom-call | tf_op jit(solution)/shard_map/update/pallas_call | solution.py:804

commit v3 on v2

--- a/solution.py
+++ b/solution.py
@@ -190,8 +190,11 @@
 
     def momentum(self, m):
         mat = self.mats[m]
-        rows, cols = mat["mom"].shape
         mat["new"][...] = MOMENTUM * mat["mom"][...] + mat["sum"][self.y, self.x] / self.group
+
+    def squares(self, m):
+        mat = self.mats[m]
+        rows, cols = mat["new"].shape
         acc = jnp.zeros((8, 128), F32)
         for i in range(0, rows, 8):
             for j in range(0, cols, 128):
@@ -310,40 +313,48 @@
                     self.ag_peer(m, f, k).wait_send()
 
 
-def reduce_kernel(side, group, ax, ga, gu, ma, mu, na, nu, xu, xa,
-                  sa, su, pa, pu, ra1, ru1, ra2, ru2, xra, slots, local_sem, send_sem, recv_sem):
-    mats = {0: dict(grad=ga, mom=ma, new=na, full=xa, sum=sa, peer=pa, ring1=ra1, ring2=ra2, own=xra),
-            1: dict(grad=gu, mom=mu, new=nu, sum=su, peer=pu, ring1=ru1, ring2=ru2, own=xu)}
+def reduce_kernel(side, group, ax, ga, gu, gd, ma, mu, md, na, nu, nd, xa,
+                  sa, su, sd, pa, pu, pd, ra1, ru1, rd1, ra2, ru2, rd2, xra, xru, xrd, slots, local_sem, send_sem, recv_sem):
+    mats = {ATTN: dict(grad=ga, mom=ma, new=na, full=xa, sum=sa, peer=pa, ring1=ra1, ring2=ra2, own=xra),
+            UP: dict(grad=gu, mom=mu, new=nu, sum=su, peer=pu, ring1=ru1, ring2=ru2, own=xru),
+            DOWN: dict(grad=gd, mom=md, new=nd, sum=sd, peer=pd, ring1=rd1, ring2=rd2, own=xrd)}
     comm = Comm(side, group, ax, mats, slots, local_sem, send_sem, recv_sem)
     pl.semaphore_wait(pltpu.get_barrier_semaphore(), comm.greet())
     comm.pair_start(ATTN)
     comm.pair_start(UP)
+    comm.pair_start(DOWN)
     comm.rs_far(ATTN)
     comm.rs_near(ATTN)
     comm.rs_own(ATTN)
     comm.pass_on(ATTN, FIRST)
+    comm.rs_far(UP)
     comm.settle(ATTN, FIRST)
+    comm.rs_near(UP)
     comm.pass_on(ATTN, SECOND)
-    comm.rs_far(UP)
+    comm.rs_own(UP)
+    comm.pass_on(UP, FIRST)
     comm.settle(ATTN, SECOND)
     comm.momentum(ATTN)
-    comm.rs_near(UP)
+    comm.squares(ATTN)
+    comm.rs_far(DOWN)
     comm.norm_x(ATTN)
-    comm.rs_own(UP)
+    comm.rs_near(DOWN)
     comm.norm_y(ATTN)
     comm.normalize(ATTN)
     comm.ag_start(ATTN)
-    comm.pass_on(UP, FIRST)
+    comm.settle(UP, FIRST)
+    comm.rs_own(DOWN)
+    comm.pass_on(DOWN, FIRST)
     comm.ag_forward(ATTN, FIRST)
+    comm.pass_on(UP, SECOND)
     comm.ag_turn(ATTN)
-    comm.settle(UP, FIRST)
-    comm.pass_on(UP, SECOND)
-    comm.ag_forward(ATTN, SECOND)
+    comm.settle(DOWN, FIRST)
     comm.settle(UP, SECOND)
     comm.momentum(UP)
-    comm.norm_x(UP)
-    comm.norm_y(UP)
-    comm.normalize(UP)
+    comm.pass_on(DOWN, SECOND)
+    comm.ag_forward(ATTN, SECOND)
+    comm.settle(DOWN, SECOND)
+    comm.momentum(DOWN)
     comm.ag_end(ATTN)
     comm.ag_arrived(ATTN)
     comm.finish()
@@ -364,29 +375,29 @@
     group = 2 * side * side
     shapes = [m.shape for m in moms]
     views = [g.reshape(side, side, 2, *s) for g, s in zip(grads, shapes)]
-    scratch = scratch_for(side, shapes) + [pltpu.VMEM(shapes[0], BF16)]
-    scratch += [pltpu.VMEM((2, 3, side, 8, 128), F32), dma((20,)), dma((110,)), dma((110,))]
-    na, nu, xu, xa = pl.pallas_call(
+    scratch = scratch_for(side, shapes) + [pltpu.VMEM(each, BF16) for each in shapes]
+    scratch += [pltpu.VMEM((2, 3, side, 8, 128), F32), dma((30,)), dma((130,)), dma((130,))]
+    na, nu, nd, xa = pl.pallas_call(
         functools.partial(reduce_kernel, side, group, ax),
         name="reduce_gather",
         out_shape=[jax.ShapeDtypeStruct(s, F32) for s in shapes]
-        + [jax.ShapeDtypeStruct(shapes[1], BF16), jax.ShapeDtypeStruct((side, side, 2) + shapes[0], BF16)],
-        in_specs=[hbm] * 2 + [vmem] * 2,
+        + [jax.ShapeDtypeStruct((side, side, 2) + shapes[0], BF16)],
+        in_specs=[hbm] * 3 + [vmem] * 3,
         out_specs=[vmem] * 3 + [hbm],
         scratch_shapes=scratch,
         compiler_params=pltpu.CompilerParams(collective_id=0, has_side_effects=True, vmem_limit_bytes=VMEM_LIMIT),
     )(*views, *moms)
-    return na, nu, xu, xa.reshape(group * shapes[0][0], shapes[0][1])
-
-
-def ns_kernel(n, side, group, ax, xa, xur, gd, md, oa_out, ou_out, od_out, nd, xu, xd,
-              X, A, B, stage, obuf, oa, ou, od, sd, pd, rd1, rd2, xrd, slots,
+    return na, nu, nd, xa.reshape(group * shapes[0][0], shapes[0][1])
+
+
+def ns_kernel(n, side, group, ax, xa, nu, nd, oa_out, ou_out, od_out, xu, xd,
+              X, A, B, stage, obuf, oa, ou, od, xru, xrd, slots,
               load_sem, asend, arecv, bsend, brecv, xsend, xrecv, osend, orecv, local_sem, send_sem, recv_sem):
     me = lax.axis_index(ax)
     role = lax.rem(me, 4)
     base = me - role
-    mats = {1: dict(full=xu, own=xur),
-            2: dict(grad=gd, mom=md, new=nd, full=xd, sum=sd, peer=pd, ring1=rd1, ring2=rd2, own=xrd)}
+    mats = {UP: dict(new=nu, full=xu, own=xru),
+            DOWN: dict(new=nd, full=xd, own=xrd)}
     comm = Comm(side, group, ax, mats, slots, local_sem, send_sem, recv_sem)
     blk = n // 4
     half = n // 2
@@ -399,26 +410,18 @@
     for step in range(1, 4):
         pl.semaphore_signal(barrier, inc=1, device_id=dev(base + lax.rem(role + step, 4)), device_id_type=MESH)
     pl.semaphore_wait(barrier, greeted + 3)
-    comm.pair_start(DOWN)
-    comm.ag_start(UP)
+    comm.squares(UP)
+    comm.squares(DOWN)
     steps = (
-        ("0A1", (comm.rs_far, DOWN)),
-        ("0A2", (comm.rs_near, DOWN)),
-        ("0A4", (comm.ag_forward, UP, FIRST)),
-        ("0Q1", (comm.rs_own, DOWN), (comm.pass_on, DOWN, FIRST)),
-        ("0Q3", (comm.ag_turn, UP)),
-        ("0P2", (comm.settle, DOWN, FIRST)),
-        ("0S1", (comm.pass_on, DOWN, SECOND)),
-        ("1A0", (comm.settle, DOWN, SECOND), (comm.momentum, DOWN)),
-        ("1A1", (comm.norm_x, DOWN)),
-        ("1A3", (comm.norm_y, DOWN)),
-        ("1Q0", (comm.normalize, DOWN), (comm.ag_start, DOWN)),
-        ("1Q1", (comm.ag_forward, UP, SECOND)),
-        ("1Q3", (comm.ag_forward, DOWN, FIRST)),
-        ("1P1", (comm.ag_turn, DOWN)),
-        ("1P3", (comm.ag_end, UP)),
-        ("1S3", (comm.ag_forward, DOWN, SECOND)),
-        ("2A2", (comm.ag_end, DOWN)),
+        ("0L0", (comm.norm_x, UP), (comm.norm_x, DOWN)),
+        ("0A1", (comm.norm_y, UP), (comm.norm_y, DOWN)),
+        ("0Q0", (comm.normalize, UP), (comm.ag_start, UP), (comm.normalize, DOWN), (comm.ag_start, DOWN)),
+        ("0Y0", (comm.ag_forward, UP, FIRST), (comm.ag_forward, DOWN, FIRST)),
+        ("0Y3", (comm.ag_turn, UP), (comm.ag_turn, DOWN)),
+        ("1Q2", (comm.ag_forward, UP, SECOND)),
+        ("1Y0", (comm.ag_forward, DOWN, SECOND)),
+        ("1Y1", (comm.ag_end, UP)),
+        ("1Y3", (comm.ag_end, DOWN)),
     )
 
     def run(calls):
@@ -464,7 +467,7 @@
                  for k, p in enumerate((p_own, s_own, p_peer, s_peer))]
         for cp in loads:
             cp.start()
-        for cp in loads:
+        for cp in loads[:2]:
             cp.wait()
 
         def a_copy(k, i, j):
@@ -481,14 +484,11 @@
             for k in ks:
                 a_copy(k, *a_blocks[k]).wait_recv()
 
-        def x_copy(nxt, p, j, k):
-            ref = at(X.at[nxt], p, j)
-            return pltpu.make_async_remote_copy(ref, ref, xsend.at[k, j], xrecv.at[k, j],
-                                                device_id=peer, device_id_type=MESH)
-
-        def x_wait(cur, k):
-            for j in QUAD:
-                x_copy(cur, (p_peer, s_peer)[k], j, k).wait_recv()
+        mine = pl.ds(pl.multiple_of(half * c, half), half)
+
+        def x_copy(nxt, j):
+            ref = X.at[nxt, mine, pl.ds(pl.multiple_of(j * blk, blk), blk)]
+            return pltpu.make_async_remote_copy(ref, ref, xsend.at[j], xrecv.at[j], device_id=peer, device_id_type=MESH)
 
         def b_copy(k):
             i, j = ((i1, j1), (i2, j2))[k]
@@ -501,43 +501,50 @@
             if mirror:
                 at(A, j, i)[...] = v.T
 
+        def col(j):
+            return pl.ds(pl.multiple_of(j * blk, blk), blk)
+
         def a_step(t, cur):
             xt = X.at[cur]
-            gram(xt, p_own, p_own, False)
-            tick(t, "A", 0)
+            A[mine, col(p_own)] = dot_nt(xt[mine, :], xt[rows(p_own), :]).astype(BF16)
+            at(A, p_own, s_own)[...] = at(A, s_own, p_own)[...].T
 
             @pl.when(t > 0)
             def _():
-                x_wait(cur, FIRST)
+                for j in QUAD:
+                    x_copy(cur, j).wait_recv()
             a_send(PP)
-            gram(xt, p_own, s_own, True)
+            a_send(SP)
             a_send(PS)
-            a_send(SP)
-            tick(t, "A", 1)
+            tick(t, "A", 0)
+
+            @pl.when(t == 0)
+            def _():
+                for cp in loads[2:]:
+                    cp.wait()
             gram(xt, i1, j1, True)
             a_send(C1)
             a_send(T1)
-            tick(t, "A", 2)
-
-            @pl.when(t > 0)
-            def _():
-                x_wait(cur, SECOND)
+            tick(t, "A", 1)
             gram(xt, i2, j2, True)
             a_send(C2)
             a_send(T2)
-            tick(t, "A", 3)
+            tick(t, "A", 2)
             gram(xt, s_own, s_own, False)
             a_send(SS)
-            tick(t, "A", 4)
-
-        def x_wait_send(nxt):
-            for k, p in enumerate((p_own, s_own)):
+            tick(t, "A", 3)
+
+        def sent(t, cur):
+            for k in every:
+                a_copy(k, *a_blocks[k]).wait_send()
+
+            @pl.when(t > 0)
+            def _():
                 for j in QUAD:
-                    x_copy(nxt, p, j, k).wait_send()
+                    x_copy(cur, j).wait_send()
 
         def q_block(i, j):
-            q = dot(A[rows(i), :], A[:, pl.ds(pl.multiple_of(j * blk, blk), blk)])
-            v = poly(at(A, i, j)[...], q)
+            v = poly(at(A, i, j)[...], dot(A[rows(i), :], A[:, col(j)]))
             at(B, i - 2 * c, j)[...] = v
             return v
 
@@ -545,84 +552,85 @@
             a_wait(C1, T1)
             q_block(p_own, p_own)
             tick(t, "Q", 0)
-            a_wait(C2, T2)
-            v = q_block(p_own, s_own)
-            at(B, s_own - 2 * c, p_own)[...] = v.T
+            a_wait(C2, T2, PP, PS, SP)
+            stage[FIRST] = q_block(i1, j1).T
+            b_copy(FIRST).start()
             tick(t, "Q", 1)
-            a_wait(PP, PS, SP)
-            v = q_block(i1, j1)
-            stage[FIRST] = v.T
-            b_copy(FIRST).start()
+            a_wait(SS)
+            stage[SECOND] = q_block(i2, j2).T
+            b_copy(SECOND).start()
             tick(t, "Q", 2)
-            a_wait(SS)
-            v = q_block(i2, j2)
-            stage[SECOND] = v.T
-            b_copy(SECOND).start()
+            B[:, col(s_own)] = poly(A[mine, col(s_own)], dot(A[mine, :], A[:, col(s_own)]))
+            at(B, s_own - 2 * c, p_own)[...] = at(B, p_own - 2 * c, s_own)[...].T
             tick(t, "Q", 3)
-            q_block(s_own, s_own)
-            tick(t, "Q", 4)
-            for k in every:
-                a_copy(k, *a_blocks[k]).wait_send()
-
-            @pl.when(t > 0)
-            def _():
-                x_wait_send(cur)
+            sent(t, cur)
 
         def y_step(t, cur, nxt):
             xt, xn = X.at[cur], X.at[nxt]
-            for k, p in enumerate((p_own, s_own)):
+            for k in PAIR:
                 b_copy(k).wait_recv()
 
-                @pl.loop(0, 4)
-                def _(j):
-                    cols = pl.ds(pl.multiple_of(j * blk, blk), blk)
-                    y = dot(B[rows(p - 2 * c), :], xt[:, cols])
-                    at(xn, p, j)[...] = blend(at(xt, p, j)[...], y)
-                    x_copy(nxt, p, j, k).start()
-                    tick(t, "PS"[k], j)
+            @pl.loop(0, 4)
+            def _(j):
+                xn[mine, col(j)] = blend(xt[mine, col(j)], dot(B[...], xt[:, col(j)]))
+                x_copy(nxt, j).start()
+                tick(t, "Y", j)
             for k in PAIR:
                 b_copy(k).wait_send()
 
-        @pl.loop(0, NS_STEPS - 1)
+        for where, *calls in steps:
+            if "L" in where:
+                run(calls)
+        last = NS_STEPS - 1
+
+        @pl.loop(0, NS_STEPS)
         def _(t):
             cur = lax.rem(t, 2)
-            nxt = 1 - cur
             a_step(t, cur)
-            q_step(t, cur)
-            y_step(t, cur, nxt)
-
-        last = NS_STEPS - 1
+
+            @pl.when(t < last)
+            def _():
+                q_step(t, cur)
+                y_step(t, cur, 1 - cur)
+
         cur = last % 2
-        a_step(last, cur)
         a_wait(*every)
-        for k in every:
-            a_copy(k, *a_blocks[k]).wait_send()
-        x_wait_send(cur)
+        sent(last, cur)
         own = oa.shape[0]
-        mine = pl.ds(pl.multiple_of(own * (base + 2 * c), 2 * own), 2 * own)
+        ours = pl.ds(pl.multiple_of(own * (base + 2 * c), 2 * own), 2 * own)
         for j in QUAD:
             cols = pl.ds(j * blk, blk)
-            B[0:2 * own, cols] = poly(A[mine, cols], dot(A[mine, :], A[:, cols]))
+            B[0:2 * own, cols] = poly(A[ours, cols], dot(A[ours, :], A[:, cols]))
+
+        def o_copy(k, target, j):
+            cols = pl.ds(j * blk, blk)
+            return pltpu.make_async_remote_copy(obuf.at[pl.ds(own * k, own), cols], oa.at[:, cols], osend.at[4 * k + j],
+                                                orecv.at[j], device_id=dev(target), device_id_type=MESH)
+
         for j in QUAD:
             cols = pl.ds(j * blk, blk)
-            obuf[0:2 * own, cols] = blend(X[cur, mine, cols], dot(B[0:2 * own, :], X[cur, :, cols]))
-
-        def o_copy(k, target):
-            return pltpu.make_async_remote_copy(obuf.at[pl.ds(own * k, own)], oa, osend.at[k], orecv.at[0],
-                                                device_id=dev(target), device_id_type=MESH)
+            obuf[0:2 * own, cols] = blend(X[cur, ours, cols], dot(B[0:2 * own, :], X[cur, :, cols]))
+
+            @pl.when(c == 1)
+            def _():
+                o_copy(FIRST, base + 2, j).start()
+                o_copy(SECOND, base + 3, j).start()
+
+            @pl.when(c == 0)
+            def _():
+                o_copy(SECOND, base + 1, j).start()
 
         @pl.when(c == 1)
         def _():
-            o_copy(0, base + 2).start()
-            o_copy(1, base + 3).start()
-            o_copy(0, base + 2).wait_send()
-            o_copy(1, base + 3).wait_send()
+            for j in QUAD:
+                o_copy(FIRST, base + 2, j).wait_send()
+                o_copy(SECOND, base + 3, j).wait_send()
 
         @pl.when(c == 0)
         def _():
-            o_copy(1, base + 1).start()
             oa[...] = obuf[0:own, :]
-            o_copy(1, base + 1).wait_send()
+            for j in QUAD:
+                o_copy(SECOND, base + 1, j).wait_send()
 
     @pl.when(role >= 2)
     def _():
@@ -654,51 +662,45 @@
         def _():
             load(xd, lambda rows_at: X.at[0, rows_at])
 
-        pairs = ((0, 0), (0, 1), (1, 1))
-
         def a_step(cur):
-            for i, j in pairs:
-                v = dot_nt(X[cur, i * blk:(i + 1) * blk, :], X[cur, j * blk:(j + 1) * blk, :]).astype(BF16)
-                at(A, i, j)[...] = v
-                if i != j:
-                    at(A, j, i)[...] = v.T
+            A[0:half, 0:blk] = dot_nt(X[cur, 0:half, :], X[cur, 0:blk, :]).astype(BF16)
+            A[0:blk, blk:half] = A[blk:half, 0:blk].T
+            A[blk:half, blk:half] = dot_nt(X[cur, blk:half, :], X[cur, blk:half, :]).astype(BF16)
 
         def q_step():
-            for i, j in pairs:
-                v = poly(at(A, i, j)[...], dot(A[i * blk:(i + 1) * blk, 0:half], A[0:half, j * blk:(j + 1) * blk]))
-                at(B, i, j)[...] = v
-                if i != j:
-                    at(B, j, i)[...] = v.T
-
-        @pl.loop(0, NS_STEPS - 1)
+            B[0:half, 0:blk] = poly(A[0:half, 0:blk], dot(A[0:half, 0:half], A[0:half, 0:blk]))
+            B[0:blk, blk:half] = B[blk:half, 0:blk].T
+            B[blk:half, blk:half] = poly(A[blk:half, blk:half], dot(A[blk:half, 0:half], A[0:half, blk:half]))
+
+        @pl.loop(0, NS_STEPS)
         def _(t):
             cur = lax.rem(t, 2)
-            nxt = 1 - cur
             a_step(cur)
 
-            q_step()
-
-            @pl.loop(0, 4)
-            def _(j):
-                cols = pl.ds(pl.multiple_of(j * blk, blk), blk)
-                for i in PAIR:
-                    y = dot(B[i * blk:(i + 1) * blk, 0:half], X[cur, 0:half, cols])
-                    at(X.at[nxt], i, j)[...] = blend(at(X.at[cur], i, j)[...], y)
+            @pl.when(jnp.logical_or(t < NS_STEPS - 1, role == 2))
+            def _():
+                q_step()
+
+            @pl.when(t < NS_STEPS - 1)
+            def _():
+                @pl.loop(0, 4)
+                def _(j):
+                    cols = pl.ds(pl.multiple_of(j * blk, blk), blk)
+                    y = dot(B[0:half, 0:half], X[cur, 0:half, cols])
+                    X[1 - cur, 0:half, cols] = blend(X[cur, 0:half, cols], y)
 
         cur = (NS_STEPS - 1) % 2
-        a_step(cur)
 
         @pl.when(role == 2)
         def _():
             own = ou.shape[0]
             cols = pl.ds(pl.multiple_of(own * base, 4 * own), 4 * own)
-            q_step()
             for i in PAIR:
                 o = blend(X[cur, i * blk:(i + 1) * blk, cols], dot(B[i * blk:(i + 1) * blk, 0:half], X[cur, 0:half, cols]))
                 obuf[0:4 * own, i * blk:(i + 1) * blk] = o.T
 
             def o_copy(k):
-                return pltpu.make_async_remote_copy(obuf.at[pl.ds(own * k, own), pl.ds(0, half)], ou, osend.at[k], orecv.at[1],
+                return pltpu.make_async_remote_copy(obuf.at[pl.ds(own * k, own), pl.ds(0, half)], ou, osend.at[k], orecv.at[4],
                                                     device_id=dev(base + k), device_id_type=MESH)
             for k in (0, 1, 3):
                 o_copy(k).start()
@@ -718,7 +720,7 @@
                 obuf[0:4 * own, cols] = blend(X[cur, mine, cols], dot(B[0:4 * own, 0:half], X[cur, 0:half, cols]))
 
             def o_copy(k):
-                return pltpu.make_async_remote_copy(obuf.at[pl.ds(own * k, own)], od, osend.at[k], orecv.at[2],
+                return pltpu.make_async_remote_copy(obuf.at[pl.ds(own * k, own)], od, osend.at[k], orecv.at[5],
                                                     device_id=dev(base + k), device_id_type=MESH)
             for k in (0, 1, 2):
                 o_copy(k).start()
@@ -731,31 +733,32 @@
 
     @pl.when(role != 3)
     def _():
-        arrived(od, 2)
+        arrived(od, 5)
     od_out[...] = od[...]
 
     @pl.when(role != 2)
     def _():
-        arrived(ou, 1)
+        arrived(ou, 4)
     ou_out[...] = ou[...]
 
     @pl.when(role != 0)
     def _():
-        arrived(oa, 0)
+        for j in QUAD:
+            arrived(oa.at[:, pl.ds(j * blk, blk)], j)
     oa_out[...] = oa[...]
     comm.finish()
     comm.ag_finish(UP)
     comm.ag_finish(DOWN)
 
 
-def orthogonalize(side, ax, xa, xu, grad_down, mom_down):
+def orthogonalize(side, ax, xa, mom_up, mom_down):
     n = xa.shape[1]
     blk = n // 4
     group = 2 * side * side
     dma = pltpu.SemaphoreType.DMA
     vmem = pl.BlockSpec(memory_space=pltpu.VMEM)
     hbm = pl.BlockSpec(memory_space=pl.ANY)
-    own_a, own_u, own_d = (n // group, n), xu.shape, mom_down.shape
+    own_a, own_u, own_d = (n // group, n), mom_up.shape, mom_down.shape
     scratch = [
         pltpu.VMEM((2, n, n), BF16),
         pltpu.VMEM((n, n), BF16),
@@ -766,21 +769,20 @@
         pltpu.VMEM(own_u, BF16),
         pltpu.VMEM(own_d, BF16),
     ]
-    scratch += scratch_for(side, [own_d]) + [pltpu.VMEM(own_d, BF16), pltpu.VMEM((3, 3, side, 8, 128), F32)]
-    scratch += [dma((group,)), dma((8,)), dma((8,)), dma((2,)), dma((2,)), dma((2, 4)), dma((2, 4)), dma((4,)), dma((3,))]
-    scratch += [dma((20,)), dma((90,)), dma((90,))]
-    oa, ou, od, nd, _, _ = pl.pallas_call(
+    scratch += [pltpu.VMEM(own_u, BF16), pltpu.VMEM(own_d, BF16), pltpu.VMEM((3, 3, side, 8, 128), F32)]
+    scratch += [dma((group,)), dma((8,)), dma((8,)), dma((2,)), dma((2,)), dma((4,)), dma((4,)), dma((8,)), dma((6,))]
+    scratch += [dma((20,)), dma((110,)), dma((110,))]
+    oa, ou, od, _, _ = pl.pallas_call(
         functools.partial(ns_kernel, n, side, group, ax),
         name="newton_schulz",
         out_shape=[jax.ShapeDtypeStruct(s, BF16) for s in (own_a, own_u, own_d)]
-        + [jax.ShapeDtypeStruct(own_d, F32)]
         + [jax.ShapeDtypeStruct((side, side, 2) + s, BF16) for s in (own_u, own_d)],
-        in_specs=[hbm, vmem, hbm, vmem],
-        out_specs=[vmem] * 4 + [hbm] * 2,
+        in_specs=[hbm, vmem, vmem],
+        out_specs=[vmem] * 3 + [hbm] * 2,
         scratch_shapes=scratch,
         compiler_params=pltpu.CompilerParams(collective_id=1, has_side_effects=True, vmem_limit_bytes=VMEM_LIMIT),
-    )(xa, xu, grad_down.reshape(side, side, 2, *own_d), mom_down)
-    return oa, ou, od, nd
+    )(xa, mom_up, mom_down)
+    return oa, ou, od
 
 
 def update_kernel(scales, *refs):
@@ -818,8 +820,8 @@
         grads = [arrays[3 * k][0, 0] for k in range(3)]
         moms = [arrays[3 * k + 1][0] for k in range(3)]
         masters = [arrays[3 * k + 2][0] for k in range(3)]
-        na, nu, xu, xa = reduce_and_gather(side, ax, grads[:2], moms[:2])
-        oa, ou, od, nd = orthogonalize(side, ax, xa, xu, grads[2], moms[2])
+        na, nu, nd, xa = reduce_and_gather(side, ax, grads, moms)
+        oa, ou, od = orthogonalize(side, ax, xa, nu, nd)
         return tuple(r[None] for r in update(group, (oa, ou, od), (na, nu, nd), masters))
 
     return jax.shard_map(step_local, mesh=mesh, in_specs=(grad_spec, row_spec, row_spec) * 3,

time: 264 us -> 258 us (0.977); the launches traced: 261 us -> 258 us
    pallas_call x1, Pallas kernels: 138 us -> 124 us  [orthogonalize(): pl.pallas_call(functools.partial(ns_kernel, n, side, group, ax), name='ne...]
    pallas_call x1, Pallas kernels: 118 us -> 130 us  [reduce_and_gather(): pl.pallas_call(functools.partial(reduce_kernel, side, group, ax), name='r...]
where the time goes in v3:
time: 258 us
  Pallas kernels  258 us (100%)
    pallas_call x1, Pallas kernels, reduce_and_gather(): pl.pallas_call(functools.partial(reduce_kernel, side, group, ax), name='r...  130 us
    pallas_call x1, Pallas kernels, orthogonalize(): pl.pallas_call(functools.partial(ns_kernel, n, side, group, ax), name='ne...  124 us

profile of v3, /device:TPU:97, one launch (start us, length us, event | category | flops | bytes accessed | tf_op | source)
XLA Modules:
  0.0 258.3 jit_solution(7219142422973469568)
XLA Ops:
  0.6 130.3 %reduce_gather.1 = (f32[64,2048]{1,0:T(8,128)}, f32[64,1024]{1,0:T(8,128)}, f32[32,2048]{1,0:T(8,128)}, bf16[4,4,2,64,2048]{4,3,2,1,0:T(8,128)(2,1)}) custom-call(f32[4,4,2,64,2048]{4,3,2,1,0:T(8,128)} %bitcast.19, f32[4,4,2,64,1024]{4,3,2,1,0:T(8,128)} %bitcast.21, f32[4,4,2,32,2048]{4,3,2,1,0:T(8,128)} %bitcast.22, f32[64,2048]{1,0:T(8,128)} %bitcast.23, ...), custom_call_target="tpu_custom_call" | custom-call | tf_op jit(solution)/shard_map/reduce_gather/pallas_call | solution.py:380
  130.9 124.1 %newton_schulz.1 = (bf16[64,2048]{1,0:T(8,128)(2,1)}, bf16[64,1024]{1,0:T(8,128)(2,1)}, bf16[32,2048]{1,0:T(8,128)(2,1)}, bf16[4,4,2,64,1024]{4,3,2,1,0:T(8,128)(2,1)}, bf16[4,4,2,32,2048]{4,3,2,1,0:T(8,128)(2,1)}) custom-call(bf16[2048,2048]{1,0:T(8,128)(2,1)} %bitcast.20, f32[64,1024]{1,0:T(8,128)} %get-tuple-element.26.nu.refs_4_, ...), custom_call_target="tpu_custom_call" | custom-call | tf_op jit(solution)/shard_map/newton_schulz/pallas_call | solution.py:775
  255.0 3.3 %update.1 = (f32[64,2048]{1,0:T(8,128)}, f32[64,2048]{1,0:T(8,128)}, bf16[64,2048]{1,0:T(8,128)(2,1)}, f32[64,1024]{1,0:T(8,128)}, f32[64,1024]{1,0:T(8,128)}, /...) custom-call(bf16[64,2048]{1,0:T(8,128)(2,1)} %get-tuple-element.28.refs_0_, ...), custom_call_target="tpu_custom_call" | custom-call | tf_op jit(solution)/shard_map/update/pallas_call | solution.py:806

commit v4 on v3

--- a/solution.py
+++ b/solution.py
@@ -86,9 +86,6 @@
     def lane1(f, k):
         return (ALL, k) if f == 0 else (k, ALL)
 
-    def lane2(self, f, k):
-        return (k, self.x) if f == 0 else (self.y, k)
-
     @staticmethod
     def one(f, k, i):
         return (i, k) if f == 0 else (k, i)
@@ -128,25 +125,30 @@
     def ring(self, m, f, phase, j):
         k, h, step = ((2, 1, 1), (2, 0, -1), (1, 0, 1), (-1, 1, -1), (1, 1, 1), (-1, 0, -1))[j]
         kk = self.shift(self.pos[f][phase], k % self.side)
-        idx = (self.lane1, self.lane2)[phase](f, kk) + (ALL, self.quarter(m, f, h))
         mat = self.mats[m]
-        return self.remote(("ring", m, f, phase, j), mat["sum"].at[idx], mat[("ring1", "ring2")[phase]].at[f, j],
+        src = self.part(m, f, kk, h) if phase else mat["sum"].at[self.lane1(f, kk) + (ALL, self.quarter(m, f, h))]
+        return self.remote(("ring", m, f, phase, j), src, mat[("ring1", "ring2")[phase]].at[f, j],
                            self.to((f == 0) == (phase == 0), step))
+
+    def part(self, m, f, k, h):
+        q = self.mats[m]["own"].shape[-1] // 4
+        return self.mats[m]["line"].at[f, k, :, pl.ds(h * q, q)]
 
     def ring_add(self, m, f, phase, j, k, h):
         self.ring(m, f, phase, j).wait_recv()
         kk = self.shift(self.pos[f][phase], k % self.side)
         cols = self.quarter(m, f, h)
         mat = self.mats[m]
-        total = mat["sum"]
         if phase == 0:
+            total = mat["sum"]
+
             @pl.loop(0, self.side)
             def _(i):
                 idx = self.one(f, kk, i) + (ALL, cols)
                 total[idx] = total[idx] + mat["ring1"][f, j, i]
         else:
-            idx = self.lane2(f, kk) + (ALL, cols)
-            total[idx] = total[idx] + mat["ring2"][f, j]
+            ref = self.part(m, f, kk, h)
+            ref[...] = ref[...] + mat["ring2"][f, j]
 
     def rs_far(self, m):
         for f in PAIR:
@@ -174,11 +176,29 @@
 
     def settle(self, m, phase):
         for f in PAIR:
-            for j, h in ((2, 0), (3, 1), (4, 1), (5, 0)):
-                self.ring_add(m, f, phase, j, 0, h)
-            if phase == 0:
-                for j in range(4):
-                    self.start(self.ring, m, f, 1, j)
+            for h, pair in enumerate(((2, 5), (3, 4))):
+                if phase:
+                    for j in pair:
+                        self.ring_add(m, f, phase, j, 0, h)
+                    continue
+                for j in pair:
+                    self.ring(m, f, phase, j).wait_recv()
+                self.line_up(m, f, h, pair)
+
+    def line_up(self, m, f, h, pair):
+        mat = self.mats[m]
+        here = self.pos[f][0]
+        left, right = pair
+
+        @pl.loop(0, self.side)
+        def _(i):
+            held = mat["sum"][self.one(f, here, i) + (ALL, self.quarter(m, f, h))]
+            self.part(m, f, i, h)[...] = held + mat["ring1"][f, left, i] + mat["ring1"][f, right, i]
+
+    def turn(self, m):
+        for f in PAIR:
+            for j in QUAD:
+                self.start(self.ring, m, f, SECOND, j)
 
     def norm_pair(self, m):
         ref = self.slots.at[m, 0, self.c]
@@ -190,7 +210,9 @@
 
     def momentum(self, m):
         mat = self.mats[m]
-        mat["new"][...] = MOMENTUM * mat["mom"][...] + mat["sum"][self.y, self.x] / self.group
+        for f in PAIR:
+            cols = self.half(m, f)
+            mat["new"][:, cols] = MOMENTUM * mat["mom"][:, cols] + mat["line"][f, self.pos[f][1]] / self.group
 
     def squares(self, m):
         mat = self.mats[m]
@@ -313,11 +335,11 @@
                     self.ag_peer(m, f, k).wait_send()
 
 
-def reduce_kernel(side, group, ax, ga, gu, gd, ma, mu, md, na, nu, nd, xa,
-                  sa, su, sd, pa, pu, pd, ra1, ru1, rd1, ra2, ru2, rd2, xra, xru, xrd, slots, local_sem, send_sem, recv_sem):
-    mats = {ATTN: dict(grad=ga, mom=ma, new=na, full=xa, sum=sa, peer=pa, ring1=ra1, ring2=ra2, own=xra),
-            UP: dict(grad=gu, mom=mu, new=nu, sum=su, peer=pu, ring1=ru1, ring2=ru2, own=xru),
-            DOWN: dict(grad=gd, mom=md, new=nd, sum=sd, peer=pd, ring1=rd1, ring2=rd2, own=xrd)}
+def reduce_kernel(side, group, ax, ga, gu, gd, ma, na, lu, ld, xa,
+                  sa, su, sd, pa, pu, pd, ra1, ru1, rd1, ra2, la, xra, xru, xrd, slots, local_sem, send_sem, recv_sem):
+    mats = {ATTN: dict(grad=ga, mom=ma, new=na, full=xa, sum=sa, peer=pa, ring1=ra1, ring2=ra2, line=la, own=xra),
+            UP: dict(grad=gu, line=lu, sum=su, peer=pu, ring1=ru1, own=xru),
+            DOWN: dict(grad=gd, line=ld, sum=sd, peer=pd, ring1=rd1, own=xrd)}
     comm = Comm(side, group, ax, mats, slots, local_sem, send_sem, recv_sem)
     pl.semaphore_wait(pltpu.get_barrier_semaphore(), comm.greet())
     comm.pair_start(ATTN)
@@ -329,6 +351,7 @@
     comm.pass_on(ATTN, FIRST)
     comm.rs_far(UP)
     comm.settle(ATTN, FIRST)
+    comm.turn(ATTN)
     comm.rs_near(UP)
     comm.pass_on(ATTN, SECOND)
     comm.rs_own(UP)
@@ -346,26 +369,17 @@
     comm.rs_own(DOWN)
     comm.pass_on(DOWN, FIRST)
     comm.ag_forward(ATTN, FIRST)
-    comm.pass_on(UP, SECOND)
     comm.ag_turn(ATTN)
     comm.settle(DOWN, FIRST)
-    comm.settle(UP, SECOND)
-    comm.momentum(UP)
-    comm.pass_on(DOWN, SECOND)
     comm.ag_forward(ATTN, SECOND)
-    comm.settle(DOWN, SECOND)
-    comm.momentum(DOWN)
     comm.ag_end(ATTN)
     comm.ag_arrived(ATTN)
     comm.finish()
     comm.ag_finish(ATTN)
 
 
-def scratch_for(side, shapes):
-    scratch = [pltpu.VMEM((side, side) + s, F32) for s in shapes] * 2
-    scratch += [pltpu.VMEM((2, 6, side, s[0], s[1] // 4), F32) for s in shapes]
-    scratch += [pltpu.VMEM((2, 6, s[0], s[1] // 4), F32) for s in shapes]
-    return scratch
+def line_shape(side, rows, cols):
+    return 2, side, rows, cols // 2
 
 
 def reduce_and_gather(side, ax, grads, moms):
@@ -375,29 +389,34 @@
     group = 2 * side * side
     shapes = [m.shape for m in moms]
     views = [g.reshape(side, side, 2, *s) for g, s in zip(grads, shapes)]
-    scratch = scratch_for(side, shapes) + [pltpu.VMEM(each, BF16) for each in shapes]
+    attn = shapes[ATTN]
+    scratch = [pltpu.VMEM((side, side) + each, F32) for each in shapes] * 2
+    scratch += [pltpu.VMEM((2, 6, side, each[0], each[1] // 4), F32) for each in shapes]
+    scratch += [pltpu.VMEM((2, 6, attn[0], attn[1] // 4), F32), pltpu.VMEM(line_shape(side, *attn), F32)]
+    scratch += [pltpu.VMEM(each, BF16) for each in shapes]
     scratch += [pltpu.VMEM((2, 3, side, 8, 128), F32), dma((30,)), dma((130,)), dma((130,))]
-    na, nu, nd, xa = pl.pallas_call(
+    na, lu, ld, xa = pl.pallas_call(
         functools.partial(reduce_kernel, side, group, ax),
         name="reduce_gather",
-        out_shape=[jax.ShapeDtypeStruct(s, F32) for s in shapes]
-        + [jax.ShapeDtypeStruct((side, side, 2) + shapes[0], BF16)],
-        in_specs=[hbm] * 3 + [vmem] * 3,
+        out_shape=[jax.ShapeDtypeStruct(attn, F32)]
+        + [jax.ShapeDtypeStruct(line_shape(side, *each), F32) for each in shapes[1:]]
+        + [jax.ShapeDtypeStruct((side, side, 2) + attn, BF16)],
+        in_specs=[hbm] * 3 + [vmem],
         out_specs=[vmem] * 3 + [hbm],
         scratch_shapes=scratch,
         compiler_params=pltpu.CompilerParams(collective_id=0, has_side_effects=True, vmem_limit_bytes=VMEM_LIMIT),
-    )(*views, *moms)
-    return na, nu, nd, xa.reshape(group * shapes[0][0], shapes[0][1])
-
-
-def ns_kernel(n, side, group, ax, xa, nu, nd, oa_out, ou_out, od_out, xu, xd,
-              X, A, B, stage, obuf, oa, ou, od, xru, xrd, slots,
+    )(*views, moms[ATTN])
+    return na, lu, ld, xa.reshape(group * shapes[0][0], shapes[0][1])
+
+
+def ns_kernel(n, side, group, ax, xa, lu_in, ld_in, mu, md, oa_out, ou_out, od_out, nu, nd, xu, xd,
+              X, A, B, stage, obuf, oa, ou, od, lu, ld, ru2, rd2, xru, xrd, slots,
               load_sem, asend, arecv, bsend, brecv, xsend, xrecv, osend, orecv, local_sem, send_sem, recv_sem):
     me = lax.axis_index(ax)
     role = lax.rem(me, 4)
     base = me - role
-    mats = {UP: dict(new=nu, full=xu, own=xru),
-            DOWN: dict(new=nd, full=xd, own=xrd)}
+    mats = {UP: dict(mom=mu, new=nu, line=lu, ring2=ru2, full=xu, own=xru),
+            DOWN: dict(mom=md, new=nd, line=ld, ring2=rd2, full=xd, own=xrd)}
     comm = Comm(side, group, ax, mats, slots, local_sem, send_sem, recv_sem)
     blk = n // 4
     half = n // 2
@@ -410,18 +429,23 @@
     for step in range(1, 4):
         pl.semaphore_signal(barrier, inc=1, device_id=dev(base + lax.rem(role + step, 4)), device_id_type=MESH)
     pl.semaphore_wait(barrier, greeted + 3)
-    comm.squares(UP)
-    comm.squares(DOWN)
+    lu[...] = lu_in[...]
+    comm.turn(UP)
+    ld[...] = ld_in[...]
+    comm.turn(DOWN)
     steps = (
-        ("0L0", (comm.norm_x, UP), (comm.norm_x, DOWN)),
-        ("0A1", (comm.norm_y, UP), (comm.norm_y, DOWN)),
-        ("0Q0", (comm.normalize, UP), (comm.ag_start, UP), (comm.normalize, DOWN), (comm.ag_start, DOWN)),
-        ("0Y0", (comm.ag_forward, UP, FIRST), (comm.ag_forward, DOWN, FIRST)),
-        ("0Y3", (comm.ag_turn, UP), (comm.ag_turn, DOWN)),
-        ("1Q2", (comm.ag_forward, UP, SECOND)),
-        ("1Y0", (comm.ag_forward, DOWN, SECOND)),
-        ("1Y1", (comm.ag_end, UP)),
-        ("1Y3", (comm.ag_end, DOWN)),
+        ("0A0", (comm.pass_on, UP, SECOND), (comm.pass_on, DOWN, SECOND)),
+        ("0A3", (comm.settle, UP, SECOND), (comm.momentum, UP), (comm.squares, UP)),
+        ("0Q1", (comm.settle, DOWN, SECOND), (comm.momentum, DOWN), (comm.squares, DOWN)),
+        ("0Q3", (comm.norm_x, UP), (comm.norm_x, DOWN)),
+        ("0Y1", (comm.norm_y, UP), (comm.norm_y, DOWN)),
+        ("0Y3", (comm.normalize, UP), (comm.ag_start, UP), (comm.normalize, DOWN), (comm.ag_start, DOWN)),
+        ("1A2", (comm.ag_forward, UP, FIRST), (comm.ag_forward, DOWN, FIRST)),
+        ("1Q1", (comm.ag_turn, UP), (comm.ag_turn, DOWN)),
+        ("1Y2", (comm.ag_forward, UP, SECOND)),
+        ("1Y3", (comm.ag_forward, DOWN, SECOND)),
+        ("2A2", (comm.ag_end, UP)),
+        ("2Q0", (comm.ag_end, DOWN)),
     )
 
     def run(calls):
@@ -751,7 +775,7 @@
     comm.ag_finish(DOWN)
 
 
-def orthogonalize(side, ax, xa, mom_up, mom_down):
+def orthogonalize(side, ax, xa, line_up, line_down, mom_up, mom_down):
     n = xa.shape[1]
     blk = n // 4
     group = 2 * side * side
@@ -769,20 +793,23 @@
         pltpu.VMEM(own_u, BF16),
         pltpu.VMEM(own_d, BF16),
     ]
+    scratch += [pltpu.VMEM(line_shape(side, *each), F32) for each in (own_u, own_d)]
+    scratch += [pltpu.VMEM((2, 6, each[0], each[1] // 4), F32) for each in (own_u, own_d)]
     scratch += [pltpu.VMEM(own_u, BF16), pltpu.VMEM(own_d, BF16), pltpu.VMEM((3, 3, side, 8, 128), F32)]
     scratch += [dma((group,)), dma((8,)), dma((8,)), dma((2,)), dma((2,)), dma((4,)), dma((4,)), dma((8,)), dma((6,))]
     scratch += [dma((20,)), dma((110,)), dma((110,))]
-    oa, ou, od, _, _ = pl.pallas_call(
+    oa, ou, od, nu, nd, _, _ = pl.pallas_call(
         functools.partial(ns_kernel, n, side, group, ax),
         name="newton_schulz",
         out_shape=[jax.ShapeDtypeStruct(s, BF16) for s in (own_a, own_u, own_d)]
+        + [jax.ShapeDtypeStruct(s, F32) for s in (own_u, own_d)]
         + [jax.ShapeDtypeStruct((side, side, 2) + s, BF16) for s in (own_u, own_d)],
-        in_specs=[hbm, vmem, vmem],
-        out_specs=[vmem] * 3 + [hbm] * 2,
+        in_specs=[hbm] + [vmem] * 4,
+        out_specs=[vmem] * 5 + [hbm] * 2,
         scratch_shapes=scratch,
         compiler_params=pltpu.CompilerParams(collective_id=1, has_side_effects=True, vmem_limit_bytes=VMEM_LIMIT),
-    )(xa, mom_up, mom_down)
-    return oa, ou, od
+    )(xa, line_up, line_down, mom_up, mom_down)
+    return oa, ou, od, nu, nd
 
 
 def update_kernel(scales, *refs):
@@ -820,8 +847,8 @@
         grads = [arrays[3 * k][0, 0] for k in range(3)]
         moms = [arrays[3 * k + 1][0] for k in range(3)]
         masters = [arrays[3 * k + 2][0] for k in range(3)]
-        na, nu, nd, xa = reduce_and_gather(side, ax, grads, moms)
-        oa, ou, od = orthogonalize(side, ax, xa, nu, nd)
+        na, lu, ld, xa = reduce_and_gather(side, ax, grads, moms)
+        oa, ou, od, nu, nd = orthogonalize(side, ax, xa, lu, ld, *moms[1:])
         return tuple(r[None] for r in update(group, (oa, ou, od), (na, nu, nd), masters))
 
     return jax.shard_map(step_local, mesh=mesh, in_specs=(grad_spec, row_spec, row_spec) * 3,

time: 258 us -> 256 us (level)
  Pallas kernels: 258 us -> 255 us
    pallas_call x1, Pallas kernels: 130 us -> 124 us  [reduce_and_gather(): pl.pallas_call(functools.partial(reduce_kernel, side, group, ax), name='r...]
    pallas_call x1, Pallas kernels: 124 us -> 128 us  [orthogonalize(): pl.pallas_call(functools.partial(ns_kernel, n, side, group, ax), name='ne...]
where the time goes in v4:
time: 256 us
  Pallas kernels  255 us (100%)
    pallas_call x1, Pallas kernels, orthogonalize(): pl.pallas_call(functools.partial(ns_kernel, n, side, group, ax), name='ne...  128 us
    pallas_call x1, Pallas kernels, reduce_and_gather(): pl.pallas_call(functools.partial(reduce_kernel, side, group, ax), name='r...  124 us

profile of v4, /device:TPU:97, one launch (start us, length us, event | category | flops | bytes accessed | tf_op | source)
XLA Modules:
  0.0 256.2 jit_solution(6048752060966343189)
XLA Ops:
  0.6 124.3 %reduce_gather.1 = (f32[64,2048]{1,0:T(8,128)}, f32[2,4,64,512]{3,2,1,0:T(8,128)}, f32[2,4,32,1024]{3,2,1,0:T(8,128)}, bf16[4,4,2,64,2048]{4,3,2,1,0:T(8,128)(2,1)}) custom-call(f32[4,4,2,64,2048]{4,3,2,1,0:T(8,128)} %bitcast.19, f32[4,4,2,64,1024]{4,3,2,1,0:T(8,128)} %bitcast.21, f32[4,4,2,32,2048]{4,3,2,1,0:T(8,128)} %bitcast.22, f32[64,2048]{1,0:T(8,128)} %bitcast.23), custom_call_target="tpu_custom_call" | custom-call | tf_op jit(solution)/shard_map/reduce_gather/pallas_call | solution.py:398
  125.0 127.8 %newton_schulz.1 = (bf16[64,2048]{1,0:T(8,128)(2,1)}, bf16[64,1024]{1,0:T(8,128)(2,1)}, bf16[32,2048]{1,0:T(8,128)(2,1)}, f32[64,1024]{1,0:T(8,128)}, f32[32,204...) custom-call(bf16[2048,2048]{1,0:T(8,128)(2,1)} %bitcast.20, ...), custom_call_target="tpu_custom_call" | custom-call | tf_op jit(solution)/shard_map/newton_schulz/pallas_call | solution.py:801
  252.8 3.3 %update.1 = (f32[64,2048]{1,0:T(8,128)}, f32[64,2048]{1,0:T(8,128)}, bf16[64,2048]{1,0:T(8,128)(2,1)}, f32[64,1024]{1,0:T(8,128)}, f32[64,1024]{1,0:T(8,128)}, /...) custom-call(bf16[64,2048]{1,0:T(8,128)(2,1)} %get-tuple-element.30.refs_0_, ...), custom_call_target="tpu_custom_call" | custom-call | tf_op jit(solution)/shard_map/update/pallas_call | solution.py:833
